TPU v7x, 32 devices: a whole 2x2x4 slice. The times are simulated.
32 devices in a mesh: dp: 8 (over z, y), mp: 4 (over x, core).
Axes of the slice: x: 2, y: 2, z: 4, core: 2. Of those that a mesh axis runs over, the one named last changes fastest.
Arguments:
- tokens: bfloat16 [49152, 512], P('dp'), may hold values from -6 to 6
- w_uvqk: bfloat16 [512, 2048], P(None, 'mp')
- w_out: bfloat16 [512, 512], replicated, may hold values from -0.25 to 0.25
- hist_len: int32 [8, 24], P('dp'), may hold values from 64 to 256, as said below
- owner: int32 [8, 24], P('dp'), may hold values from 0 to 7, as said below
- recv_offset: int32 [8, 24], P('dp'), may hold values from 0 to 47, as said below
- block_start: int32 [8, 24], P('dp'), may hold values from 0 to 47, as said below
Outputs:
- packed_out: bfloat16 [49152, 512], P('dp', 'mp')
- user_state: bfloat16 [192, 512], P('dp', 'mp')
Inputs may be any that keep to these rules, and one draw needn't show every extreme that they name: User (d, u) has ceil(hist_len / 128) blocks, at most 2. owner[d, u] = (p(d) + r(u mod 8)) mod 8 for two permutations p, r of the indices of dp drawn from the seed: every owner receives exactly 24 users, and one device sends at most 3 users to one owner. On some owner every received user has 2 blocks. `recv_offset`: the users of one owner occupy disjoint runs of its 48 blocks, in the order of u; on some owner they fill all 48 blocks. `block_start`: the users of one device occupy disjoint runs of its 48 blocks, in the order of u.
All inputs are finite; a program needn't handle non-finite values.
Results may differ from a plain program's by a relative error of at most 0.0059.
Values may be sent and summed in bfloat16 or wider, within the bound.
A program may use at most 128 MiB of HBM per device.

v0:
```python
import functools

import jax
import jax.numpy as jnp
from jax import lax
from jax.experimental import pallas as pl
from jax.experimental.pallas import tpu as pltpu
from jax.sharding import PartitionSpec as P

D = 512
HEADS = 4
HEAD = D // HEADS
BLOCK = 128
MAXB = 2
WIN = MAXB * BLOCK
EPS = 1e-05
MESH = pl.DeviceIdType.MESH


def norm_rows(values):
    average = jnp.mean(values, axis=-1, keepdims=True)
    variance = jnp.mean(values * values, axis=-1, keepdims=True) - average * average
    return (values - average) * lax.rsqrt(variance + EPS)


def gather_kernel(
    dp_size, mp_size, per_pair,
    owner, hist_len, recv_offset, block_start, tok_hbm,
    table, user_pos, picked, row_sem,
):
    d = lax.axis_index("dp")
    m = lax.axis_index("mp")
    last_block = tok_hbm.shape[0] - 1
    slots = picked.shape[0]

    def clear(o, carry):
        for lane in range(4 * per_pair):
            table[o, 0, lane] = 0
        return carry

    lax.fori_loop(0, dp_size, clear, 0)

    def enter(u, carry):
        o = owner[0, u]
        rank = table[o, 0, 3]
        table[o, 0, 3] = rank + 1
        table[o, 0, 4 * rank] = block_start[0, u]
        table[o, 0, 4 * rank + 1] = hist_len[0, u]
        table[o, 0, 4 * rank + 2] = recv_offset[0, u]
        user_pos[u] = o * per_pair + rank
        return carry

    lax.fori_loop(0, user_pos.shape[0], enter, 0)

    def copy(s, b):
        k = s // per_pair
        o = lax.rem(d + m + mp_size * k, dp_size)
        start = table[o, 0, 4 * (s - k * per_pair)]
        return pltpu.make_async_copy(
            tok_hbm.at[jnp.minimum(start + b, last_block)], picked.at[s, b], row_sem.at[s, b]
        )

    def begin(s, carry):
        for b in range(MAXB):
            copy(s, b).start()
        return carry

    def end(s, carry):
        for b in range(MAXB):
            copy(s, b).wait()
        return carry

    lax.fori_loop(0, slots, begin, 0)
    lax.fori_loop(0, slots, end, 0)


def layer_kernel(
    dp_size, mp_size, per_pair,
    rows_ref, w_ref, wout_ref, meta_ref,
    arr, meta_out, state_in,
    xin, wg, wop, send, state_out, meta_in,
    own_sem, w_send, w_recv, meta_send, meta_recv, row_send, row_recv, send_sem, recv_sem,
    state_send, state_recv, out_sem,
):
    d = lax.axis_index("dp")
    m = lax.axis_index("mp")
    quarter = D // mp_size
    reach = dp_size // mp_size
    slots = reach * per_pair

    own_copy = pltpu.make_async_copy(w_ref, wg.at[0], own_sem)
    own_copy.start()

    barrier = pltpu.get_barrier_semaphore()

    def greet(step, carry):
        o = lax.rem(d + step // mp_size, dp_size)
        q = lax.rem(m + lax.rem(step, mp_size), mp_size)
        pl.semaphore_signal(barrier, inc=1, device_id={"dp": o, "mp": q}, device_id_type=MESH)
        return carry

    lax.fori_loop(1, dp_size * mp_size, greet, 0)
    pl.semaphore_wait(barrier, dp_size * mp_size - 1)

    def flip(bits):
        if bits == 1:
            return m + 1 - 2 * lax.rem(m, 2)
        return lax.rem(m + 2, 4)

    def w_copy(src, slot, peer, index):
        return pltpu.make_async_remote_copy(
            src_ref=src, dst_ref=wg.at[slot], send_sem=w_send.at[index],
            recv_sem=w_recv.at[index], device_id={"mp": peer}, device_id_type=MESH,
        )

    far = w_copy(w_ref, 2, flip(2), 1)
    far.start()
    near = w_copy(w_ref, 1, flip(1), 0)
    near.start()
    relay = w_copy(wg.at[2], 3, flip(1), 2)

    def target(s):
        k = s // per_pair
        return lax.rem(d + m + mp_size * k, dp_size)

    def source(s):
        k = s // per_pair
        return lax.rem(d - m - mp_size * k + 2 * dp_size, dp_size), s - k * per_pair

    def row_copy(s):
        return pltpu.make_async_remote_copy(
            src_ref=rows_ref.at[s], dst_ref=xin.at[s], send_sem=row_send.at[s],
            recv_sem=row_recv.at[s], device_id={"dp": target(s)}, device_id_type=MESH,
        )

    def row_local(s):
        return pltpu.make_async_copy(rows_ref.at[s], xin.at[s], row_recv.at[s])

    def travels(s):
        k = s // per_pair
        return s - k * per_pair == 0

    def start_rows(s, carry):
        away = jnp.logical_and(travels(s), target(s) != d)

        @pl.when(away)
        def _():
            row_copy(s).start()

        @pl.when(jnp.logical_not(away))
        def _():
            row_local(s).start()

        return carry

    def end_rows(s, carry):
        @pl.when(jnp.logical_and(travels(s), target(s) != d))
        def _():
            row_copy(s).wait_send()

        return carry

    lax.fori_loop(0, slots, start_rows, 0)

    def meta_copy(step):
        o = lax.rem(d + step, dp_size)
        return pltpu.make_async_remote_copy(
            src_ref=meta_ref.at[o], dst_ref=meta_in.at[d], send_sem=meta_send.at[step],
            recv_sem=meta_recv.at[d], device_id={"dp": o}, device_id_type=MESH,
        )

    def start_meta(step, carry):
        meta_copy(step).start()
        return carry

    lax.fori_loop(1, dp_size, start_meta, 0)
    pltpu.make_async_copy(meta_ref.at[d], meta_in.at[d], meta_recv.at[d]).start()

    for bits in range(mp_size):
        head = m
        if bits & 1:
            head = head + 1 - 2 * lax.rem(head, 2)
        if bits & 2:
            head = lax.rem(head + 2, 4)
        wop[bits * HEAD : (bits + 1) * HEAD, :] = wout_ref[
            pl.ds(pl.multiple_of(head * HEAD, HEAD), HEAD), :
        ]

    causal = lax.broadcasted_iota(jnp.int32, (BLOCK, BLOCK), 1) <= lax.broadcasted_iota(
        jnp.int32, (BLOCK, BLOCK), 0
    )
    half_scale = 0.5 * HEAD ** (-0.5)

    def scores(q, k):
        t = lax.dot_general(
            q, k, (((1,), (1,)), ((), ())), preferred_element_type=jnp.float32
        ) * half_scale
        return t + t * jnp.tanh(t)

    def one_head(rows_in, bits):
        h = jnp.dot(rows_in, wg[bits], preferred_element_type=jnp.float32) * 0.5
        p = (h + h * jnp.tanh(h)).astype(jnp.bfloat16)
        u, v, q, k = (p[:, i * HEAD : (i + 1) * HEAD] for i in range(4))
        low = jnp.where(causal, scores(q[:BLOCK], k[:BLOCK]), 0.0).astype(jnp.bfloat16)
        back = scores(q[BLOCK:], k[:BLOCK])
        diag = jnp.where(causal, scores(q[BLOCK:], k[BLOCK:]), 0.0)
        high = jnp.concatenate([back, diag], 1).astype(jnp.bfloat16)
        first = jnp.dot(low, v[:BLOCK], preferred_element_type=jnp.float32)
        second = jnp.dot(high, v, preferred_element_type=jnp.float32)
        return u, jnp.concatenate([first, second], 0) * (1.0 / WIN)

    def got_meta(src, carry):
        pltpu.make_async_copy(meta_ref.at[src], meta_in.at[src], meta_recv.at[src]).wait()
        return carry

    lax.fori_loop(0, dp_size, got_meta, 0)
    meta_back = pltpu.make_async_copy(meta_in, meta_out, out_sem)
    meta_back.start()

    own_copy.wait()
    near.wait()
    far.wait()
    relay.start()
    relay.wait()

    def route(s):
        src, j = source(s)
        moved = travels(s)
        home = jnp.where(moved, src, d)
        there = jnp.where(moved, d, target(s))
        return moved, home, there, j

    def send_copy(s, q):
        _, home, there, j = route(s)
        pair = home * per_pair + j
        return pltpu.make_async_remote_copy(
            src_ref=send.at[s, q], dst_ref=arr.at[pair], send_sem=send_sem.at[s, q],
            recv_sem=recv_sem.at[pair], device_id={"dp": there, "mp": q}, device_id_type=MESH,
        )

    def state_copy(s, q):
        _, home, there, j = route(s)
        pair = there * per_pair + j
        return pltpu.make_async_remote_copy(
            src_ref=state_out.at[s, q], dst_ref=state_in.at[pair], send_sem=state_send.at[s, q],
            recv_sem=state_recv.at[pair], device_id={"dp": home, "mp": q}, device_id_type=MESH,
        )

    picks = lax.broadcasted_iota(jnp.int32, (8, WIN), 1)
    lanes = lax.broadcasted_iota(jnp.int32, (1, 128), 1)
    positions = lax.broadcasted_iota(jnp.int32, (WIN, D), 0)

    def one_user(s):
        row_local(s).wait()
        moved, home, there, j = route(s)
        src, _ = source(s)
        rows_in = xin[s].reshape(WIN, D).astype(jnp.float32)
        n = norm_rows(rows_in).astype(jnp.bfloat16)
        parts = [one_head(n, bits) for bits in range(mp_size)]
        a = jnp.concatenate([part[1] for part in parts], 1)
        g = jnp.concatenate([part[0] for part in parts], 1).astype(jnp.float32)
        gated = (norm_rows(a) * g).astype(jnp.bfloat16)
        y = jnp.dot(gated, wop[...], preferred_element_type=jnp.float32)
        entry = jnp.where(moved, meta_in[src], meta_ref[target(s)])
        length = jnp.sum(jnp.where(lanes == 4 * j + 1, entry, 0), axis=1, keepdims=True)
        y = jnp.where(positions < length, y + rows_in, 0.0).astype(jnp.bfloat16)
        for q in range(mp_size):
            send[s, q] = y[:, q * quarter : (q + 1) * quarter]
        pick = jnp.where(picks == length - 1, 1.0, 0.0).astype(jnp.bfloat16)
        chosen = jnp.dot(pick, y, preferred_element_type=jnp.float32)
        for q in range(mp_size):
            state_out[s, q] = chosen[:, q * quarter : (q + 1) * quarter]
        pair = home * per_pair + j
        state_pair = there * per_pair + j
        for q in range(mp_size):
            own = jnp.logical_and(there == d, q == m)

            @pl.when(jnp.logical_not(own))
            def _():
                send_copy(s, q).start()

            @pl.when(own)
            def _():
                pltpu.make_async_copy(send.at[s, q], arr.at[pair], recv_sem.at[pair]).start()

        for q in range(mp_size):
            own = jnp.logical_and(home == d, q == m)

            @pl.when(jnp.logical_not(own))
            def _():
                state_copy(s, q).start()

            @pl.when(own)
            def _():
                pltpu.make_async_copy(
                    state_out.at[s, q], state_in.at[state_pair], state_recv.at[state_pair]
                ).start()

    def turn(i, carry):
        late = i // slots
        s = i - late * slots
        s = jnp.where(late == 0, slots - 1 - s, s)

        @pl.when(travels(s) == (late == 1))
        def _():
            one_user(s)

        return carry

    lax.fori_loop(0, 2 * slots, turn, 0)
    meta_back.wait()

    def end_meta(step, carry):
        meta_copy(step).wait_send()
        return carry

    lax.fori_loop(1, dp_size, end_meta, 0)
    lax.fori_loop(0, slots, end_rows, 0)

    def sent(s, carry):
        _, home, there, _ = route(s)
        for q in range(mp_size):

            @pl.when(jnp.logical_not(jnp.logical_and(there == d, q == m)))
            def _():
                send_copy(s, q).wait_send()

            @pl.when(jnp.logical_not(jnp.logical_and(home == d, q == m)))
            def _():
                state_copy(s, q).wait_send()

        return carry

    lax.fori_loop(0, slots, sent, 0)

    def got(i, carry):
        pltpu.make_async_copy(send.at[0, 0], arr.at[i], recv_sem.at[i]).wait()
        pltpu.make_async_copy(state_out.at[0, 0], state_in.at[i], state_recv.at[i]).wait()
        return carry

    lax.fori_loop(0, dp_size * per_pair, got, 0)


def place_kernel(
    dp_size, per_pair,
    meta, user_pos, arr, state_in,
    packed, state,
    held, zero, rows32, used, in_sem, out_sem,
):
    pairs = dp_size * per_pair
    blocks = packed.shape[0]

    def bring(i):
        return pltpu.make_async_copy(arr.at[i], held.at[i], in_sem.at[i])

    def put(source, block):
        return pltpu.make_async_copy(source, packed.at[block], out_sem.at[block])

    def begin(i, carry):
        bring(i).start()
        return carry

    lax.fori_loop(0, pairs, begin, 0)
    zero[...] = jnp.zeros(zero.shape, zero.dtype)
    for block in range(blocks):
        used[block] = 0

    def pick(u, carry):
        rows32[pl.ds(u, 1), :] = state_in[user_pos[u], 0:1, :]
        return carry

    lax.fori_loop(0, state.shape[0], pick, 0)
    state[...] = rows32[...].astype(state.dtype)

    def one(i, carry):
        src = i // per_pair
        j = i - src * per_pair
        length = meta[src, 0, 4 * j + 1]
        offset = meta[src, 0, 4 * j + 2]
        bring(i).wait()
        for b in range(MAXB):

            @pl.when(length > b * BLOCK)
            def _():
                used[offset + b] = 1
                put(held.at[i, pl.ds(b * BLOCK, BLOCK)], offset + b).start()

        return carry

    lax.fori_loop(0, pairs, one, 0)

    def fill(block, carry):
        @pl.when(used[block] == 0)
        def _():
            put(zero, block).start()

        return carry

    lax.fori_loop(0, blocks, fill, 0)

    def end(block, carry):
        put(zero, block).wait()
        return carry

    lax.fori_loop(0, blocks, end, 0)


def per_device(tokens, w_uvqk, w_out, hist_len, owner, recv_offset, block_start):
    dp_size = lax.axis_size("dp")
    mp_size = lax.axis_size("mp")
    user_count = hist_len.shape[1]
    per_pair = -(-user_count // dp_size)
    pairs = dp_size * per_pair
    reach = dp_size // mp_size
    slots = reach * per_pair
    quarter = D // mp_size
    rows = tokens.shape[0]

    vmem = pl.BlockSpec(memory_space=pltpu.VMEM)
    smem = pl.BlockSpec(memory_space=pltpu.SMEM)
    anywhere = pl.BlockSpec(memory_space=pl.ANY)
    bf16, f32 = jnp.bfloat16, jnp.float32
    dma = pltpu.SemaphoreType.DMA
    meta, user_pos, picked = pl.pallas_call(
        functools.partial(gather_kernel, dp_size, mp_size, per_pair),
        out_shape=(
            jax.ShapeDtypeStruct((dp_size, 1, 128), jnp.int32),
            jax.ShapeDtypeStruct((user_count,), jnp.int32),
            jax.ShapeDtypeStruct((slots, MAXB, BLOCK, D), bf16),
        ),
        in_specs=[smem, smem, smem, smem, anywhere],
        out_specs=(smem, smem, vmem),
        scratch_shapes=[dma((slots, MAXB))],
        name="gather",
    )(owner, hist_len, recv_offset, block_start, tokens.reshape(rows // BLOCK, BLOCK, D))
    arr, meta_in, state_in = pl.pallas_call(
        functools.partial(layer_kernel, dp_size, mp_size, per_pair),
        out_shape=(
            jax.ShapeDtypeStruct((pairs, WIN, quarter), bf16),
            jax.ShapeDtypeStruct((dp_size, 1, 128), jnp.int32),
            jax.ShapeDtypeStruct((pairs, 8, quarter), f32),
        ),
        in_specs=[anywhere, vmem, vmem, vmem],
        out_specs=(anywhere, anywhere, anywhere),
        scratch_shapes=[
            pltpu.VMEM((slots, MAXB, BLOCK, D), bf16),
            pltpu.VMEM((mp_size, D, 4 * HEAD), bf16),
            pltpu.VMEM((D, D), bf16),
            pltpu.VMEM((slots, mp_size, WIN, quarter), bf16),
            pltpu.VMEM((slots, mp_size, 8, quarter), f32),
            pltpu.VMEM((dp_size, 1, 128), jnp.int32),
            dma,
            dma((3,)),
            dma((3,)),
            dma((dp_size,)),
            dma((dp_size,)),
            dma((slots,)),
            dma((slots,)),
            dma((slots, mp_size)),
            dma((pairs,)),
            dma((slots, mp_size)),
            dma((pairs,)),
            dma,
        ],
        compiler_params=pltpu.CompilerParams(
            collective_id=0, has_side_effects=True, vmem_limit_bytes=60 * 1024 * 1024
        ),
        name="layer",
    )(picked, w_uvqk, w_out, meta)
    packed, state = pl.pallas_call(
        functools.partial(place_kernel, dp_size, per_pair),
        out_shape=(
            jax.ShapeDtypeStruct((rows // BLOCK, BLOCK, quarter), bf16),
            jax.ShapeDtypeStruct((user_count, quarter), bf16),
        ),
        in_specs=[smem, smem, anywhere, vmem],
        out_specs=(anywhere, vmem),
        scratch_shapes=[
            pltpu.VMEM((pairs, WIN, quarter), bf16),
            pltpu.VMEM((BLOCK, quarter), bf16),
            pltpu.VMEM((user_count, quarter), f32),
            pltpu.SMEM((rows // BLOCK,), jnp.int32),
            dma((pairs,)),
            dma((rows // BLOCK,)),
        ],
        compiler_params=pltpu.CompilerParams(vmem_limit_bytes=60 * 1024 * 1024),
        name="place",
    )(meta_in, user_pos, arr, state_in)
    return packed.reshape(rows, quarter), state


def solution(mesh):
    in_specs = (
        P("dp", None),
        P(None, "mp"),
        P(),
        P("dp", None),
        P("dp", None),
        P("dp", None),
        P("dp", None),
    )
    out_specs = (P("dp", "mp"), P("dp", "mp"))
    return jax.shard_map(
        per_device, mesh=mesh, in_specs=in_specs, out_specs=out_specs, check_vma=False
    )
```

profile of v0, /device:TPU:1, one launch (start us, length us, event | category | flops | bytes accessed | tf_op | source)
XLA Modules:
  0.0 62.8 jit_solution(14895935764784439692)
XLA Ops:
  0.6 4.0 %gather.1 = (s32[8,1,128]{2,1,0:T(1,128)}, s32[24]{0:T(128)}, bf16[6,2,128,512]{3,2,1,0:T(8,128)(2,1)}) custom-call(s32[1,24]{1,0:T(1,128)} %owner.1, s32[1,24]{1,0:T(1,128)} %hist_len.1, s32[1,24]{1,0:T(1,128)} %recv_offset.1, s32[1,24]{1,0:T(1,128)} %block_start.1, bf16[48,128,512]{2,1,0:T(8,128)(2,1)} %bitcast.2), custom_call_target="tpu_custom_call" | custom-call | tf_op jit(solution)/shard_map/gather/pallas_call | solution.py:424
  4.6 53.7 %layer.1 = (bf16[24,256,128]{2,1,0:T(8,128)(2,1)}, s32[8,1,128]{2,1,0:T(1,128)}, f32[24,8,128]{2,1,0:T(8,128)}) custom-call(bf16[6,2,128,512]{3,2,1,0:T(8,128)(2,1)} %get-tuple-element.10.rows_ref, bf16[512,512]{1,0:T(8,128)(2,1)} %w_ref.1, bf16[512,512]{1,0:T(8,128)(2,1)} %wout_ref.1, s32[8,1,128]{2,1,0:T(1,128)} %get-tuple-element.11.meta_ref), custom_call_target="tpu_custom_call" | custom-call | tf_op jit(solution)/shard_map/layer/pallas_call | solution.py:436
  58.3 4.5 %place.1 = (bf16[48,128,128]{2,1,0:T(8,128)(2,1)}, bf16[24,128]{1,0:T(8,128)(2,1)}) custom-call(s32[8,1,128]{2,1,0:T(1,128)} %get-tuple-element.12.meta, s32[24]{0:T(128)} %get-tuple-element.13.user_pos, bf16[24,256,128]{2,1,0:T(8,128)(2,1)} %get-tuple-element.14.arr, f32[24,8,128]{2,1,0:T(8,128)} %get-tuple-element.15.state_in), custom_call_target="tpu_custom_call" | custom-call | tf_op jit(solution)/shard_map/place/pallas_call | solution.py:470
where the time goes:
time: 63.5 us; the launch traced here: 62.8 us
  Pallas kernels  62.1 us (98%)
  between operations  0.65 us (1%)
    pallas_call x1, Pallas kernels, per_device(): pl.pallas_call(functools.partial(layer_kernel, dp_size, mp_size, per_pair...  53.7 us
    pallas_call x1, Pallas kernels, per_device(): pl.pallas_call(functools.partial(place_kernel, dp_size, per_pair), out_sh...  4.46 us
    pallas_call x1, Pallas kernels, per_device(): pl.pallas_call(functools.partial(gather_kernel, dp_size, mp_size, per_pai...  3.96 us

commit v1 on v0

v1 whole, which is shorter than its diff:
```python
import functools

import jax
import jax.numpy as jnp
from jax import lax
from jax.experimental import pallas as pl
from jax.experimental.pallas import tpu as pltpu
from jax.sharding import PartitionSpec as P

D = 512
HEADS = 4
HEAD = D // HEADS
BLOCK = 128
MAXB = 2
WIN = MAXB * BLOCK
EPS = 1e-05
CHUNKS = 4
MESH = pl.DeviceIdType.MESH


def norm_rows(values):
    average = jnp.mean(values, axis=-1, keepdims=True)
    variance = jnp.mean(values * values, axis=-1, keepdims=True) - average * average
    return (values - average) * lax.rsqrt(variance + EPS)


def layer_kernel(
    dp_size, mp_size, per_pair, user_count,
    tok_hbm, w_hbm, wout_hbm, owner_hbm, len_hbm, off_hbm, start_hbm,
    packed, state,
    tok, buf, wg, wop, send, state_out, arr, state_in, state32, meta_my, meta_in, inv_v,
    owner_s, len_s, off_s, start_s, meta_s, inv_s,
    tab_sem, tok_sem, w_sem, wop_sem, w_send, w_recv, meta_send, meta_recv, row_send, row_recv,
    send_sem, recv_sem, state_send, state_recv, local_sem,
):
    d = lax.axis_index("dp")
    m = lax.axis_index("mp")
    quarter = D // mp_size
    reach = dp_size // mp_size
    slots = reach * per_pair
    pairs = dp_size * per_pair
    blocks = packed.shape[0]
    last_block = tok_hbm.shape[0] - 1
    barrier = pltpu.get_barrier_semaphore()

    def greet(step, carry):
        o = lax.rem(d + step // mp_size, dp_size)
        q = lax.rem(m + lax.rem(step, mp_size), mp_size)
        pl.semaphore_signal(barrier, inc=1, device_id={"dp": o, "mp": q}, device_id_type=MESH)
        return carry

    tables = [
        pltpu.make_async_copy(src, dst, tab_sem.at[i])
        for i, (src, dst) in enumerate(
            ((owner_hbm, owner_s), (len_hbm, len_s), (off_hbm, off_s), (start_hbm, start_s))
        )
    ]
    for table in tables:
        table.start()
    tok_copy = pltpu.make_async_copy(tok_hbm, tok, tok_sem)
    tok_copy.start()
    own_w = pltpu.make_async_copy(w_hbm, wg.at[0], w_sem)
    own_w.start()
    lax.fori_loop(1, dp_size * mp_size, greet, 0)

    def flip(bits):
        if bits == 1:
            return m + 1 - 2 * lax.rem(m, 2)
        return lax.rem(m + 2, 4)

    wop_copies = []
    for bits in range(mp_size):
        head = m
        if bits & 1:
            head = head + 1 - 2 * lax.rem(head, 2)
        if bits & 2:
            head = lax.rem(head + 2, 4)
        copy = pltpu.make_async_copy(
            wout_hbm.at[pl.ds(pl.multiple_of(head * HEAD, HEAD), HEAD)],
            wop.at[pl.ds(bits * HEAD, HEAD)], wop_sem.at[bits],
        )
        copy.start()
        wop_copies.append(copy)

    def target(s):
        k = s // per_pair
        return lax.rem(d + m + mp_size * k, dp_size)

    def source(s):
        k = s // per_pair
        return lax.rem(d - m - mp_size * k + 2 * dp_size, dp_size), s - k * per_pair

    def moves(s):
        k = s // per_pair
        j = s - k * per_pair
        return jnp.logical_and(j < 1 + lax.rem(m, 2), target(s) != d)

    def crosses(s):
        return (target(s) < dp_size // 2) != (d < dp_size // 2)

    def find(o):
        first = 0
        found = 0
        for u in range(min(dp_size, user_count)):
            hit = owner_s[0, u] == o
            first = jnp.where(hit, u, first)
            found = jnp.where(hit, 1, found)
        return first, found

    def user_of(o, j):
        first, found = find(o)
        u = first + j * dp_size
        valid = jnp.logical_and(found == 1, u < user_count)
        return jnp.minimum(u, user_count - 1), valid

    for table in tables:
        table.wait()

    lanes = lax.broadcasted_iota(jnp.int32, (1, 128), 1)

    def fill_meta(o, carry):
        first, found = find(o)
        row = jnp.zeros((1, 128), jnp.int32)
        for j in range(per_pair):
            u = first + j * dp_size
            valid = jnp.logical_and(found == 1, u < user_count)
            u = jnp.minimum(u, user_count - 1)
            row = jnp.where(lanes == 2 * j, jnp.where(valid, len_s[0, u], 0), row)
            row = jnp.where(lanes == 2 * j + 1, off_s[0, u], row)
        meta_my[o] = row
        return carry

    lax.fori_loop(0, dp_size, fill_meta, 0)
    meta_in[d] = meta_my[d]
    zero_block = 2 * pairs
    arr[zero_block] = jnp.zeros((BLOCK, quarter), arr.dtype)
    tok_copy.wait()

    def stage(s):
        k = s // per_pair
        u, _ = user_of(target(s), s - k * per_pair)
        start = start_s[0, u]
        for b in range(MAXB):
            buf[0, s, b] = tok[jnp.minimum(start + b, last_block)]

    def stage_moved(s, carry):
        @pl.when(moves(s))
        def _():
            stage(s)

        return carry

    def stage_home(s, carry):
        @pl.when(jnp.logical_not(moves(s)))
        def _():
            stage(s)

        return carry

    lax.fori_loop(0, slots, stage_moved, 0)
    own_w.wait()

    pl.semaphore_wait(barrier, dp_size * mp_size - 1)

    def meta_copy(step):
        o = lax.rem(d + step, dp_size)
        return pltpu.make_async_remote_copy(
            src_ref=meta_my.at[o], dst_ref=meta_in.at[d], send_sem=meta_send.at[step],
            recv_sem=meta_recv.at[d], device_id={"dp": o}, device_id_type=MESH,
        )

    def start_meta(step, carry):
        meta_copy(step).start()
        return carry

    lax.fori_loop(1, dp_size, start_meta, 0)

    def row_copy(s):
        return pltpu.make_async_remote_copy(
            src_ref=buf.at[0, s], dst_ref=buf.at[1, s], send_sem=row_send.at[s],
            recv_sem=row_recv.at[s], device_id={"dp": target(s)}, device_id_type=MESH,
        )

    def row_local(s):
        return pltpu.make_async_copy(buf.at[0, s], buf.at[1, s], row_recv.at[s])

    def start_rows(i, carry):
        late = i // slots
        s = i - late * slots

        @pl.when(jnp.logical_and(moves(s), crosses(s) == (late == 0)))
        def _():
            row_copy(s).start()

        return carry

    lax.fori_loop(0, 2 * slots, start_rows, 0)

    piece = D // CHUNKS

    def w_copy(src, dst, chunk, peer, index):
        rows = pl.ds(chunk * piece, piece)
        return pltpu.make_async_remote_copy(
            src_ref=wg.at[src, rows], dst_ref=wg.at[dst, rows], send_sem=w_send.at[index, chunk],
            recv_sem=w_recv.at[index, chunk], device_id={"mp": peer}, device_id_type=MESH,
        )

    far = [w_copy(0, 2, c, flip(2), 1) for c in range(CHUNKS)]
    near = [w_copy(0, 1, c, flip(1), 0) for c in range(CHUNKS)]
    relay = [w_copy(2, 3, c, flip(1), 2) for c in range(CHUNKS)]
    for copy in far:
        copy.start()
    for copy in near:
        copy.start()

    lax.fori_loop(0, slots, stage_home, 0)

    causal = lax.broadcasted_iota(jnp.int32, (BLOCK, BLOCK), 1) <= lax.broadcasted_iota(
        jnp.int32, (BLOCK, BLOCK), 0
    )
    half_scale = 0.5 * HEAD ** (-0.5)

    def scores(q, k):
        t = lax.dot_general(
            q, k, (((1,), (1,)), ((), ())), preferred_element_type=jnp.float32
        ) * half_scale
        return t + t * jnp.tanh(t)

    def one_head(rows_in, bits):
        h = jnp.dot(rows_in, wg[bits], preferred_element_type=jnp.float32) * 0.5
        p = (h + h * jnp.tanh(h)).astype(jnp.bfloat16)
        u, v, q, k = (p[:, i * HEAD : (i + 1) * HEAD] for i in range(4))
        low = jnp.where(causal, scores(q[:BLOCK], k[:BLOCK]), 0.0).astype(jnp.bfloat16)
        back = scores(q[BLOCK:], k[:BLOCK])
        diag = jnp.where(causal, scores(q[BLOCK:], k[BLOCK:]), 0.0)
        high = jnp.concatenate([back, diag], 1).astype(jnp.bfloat16)
        first = jnp.dot(low, v[:BLOCK], preferred_element_type=jnp.float32)
        second = jnp.dot(high, v, preferred_element_type=jnp.float32)
        return u, jnp.concatenate([first, second], 0) * (1.0 / WIN)

    for copy in wop_copies:
        copy.wait()
    for copy in near:
        copy.wait()
    for c in range(CHUNKS):
        far[c].wait()
        relay[c].start()
    for c in range(CHUNKS):
        relay[c].wait()

    def route(s):
        src, j = source(s)
        moved = moves(s)
        home = jnp.where(moved, src, d)
        there = jnp.where(moved, d, target(s))
        return moved, home, there, j

    def send_copy(s, q):
        _, home, there, j = route(s)
        pair = home * per_pair + j
        return pltpu.make_async_remote_copy(
            src_ref=send.at[s, q], dst_ref=arr.at[pl.ds(MAXB * pair, MAXB)],
            send_sem=send_sem.at[s, q], recv_sem=recv_sem.at[pair],
            device_id={"dp": there, "mp": q}, device_id_type=MESH,
        )

    def send_local(s, q, pair):
        return pltpu.make_async_copy(
            send.at[s, q], arr.at[pl.ds(MAXB * pair, MAXB)], recv_sem.at[pair]
        )

    def state_copy(s, q):
        _, home, there, j = route(s)
        pair = there * per_pair + j
        return pltpu.make_async_remote_copy(
            src_ref=state_out.at[s, q], dst_ref=state_in.at[pair], send_sem=state_send.at[s, q],
            recv_sem=state_recv.at[pair], device_id={"dp": home, "mp": q}, device_id_type=MESH,
        )

    def state_local(s, q, pair):
        return pltpu.make_async_copy(state_out.at[s, q], state_in.at[pair], state_recv.at[pair])

    picks = lax.broadcasted_iota(jnp.int32, (8, WIN), 1)
    positions = lax.broadcasted_iota(jnp.int32, (WIN, D), 0)

    def one_user(s, length):
        moved, home, there, j = route(s)
        rows_in = buf[jnp.where(moved, 1, 0), s].reshape(WIN, D).astype(jnp.float32)
        n = norm_rows(rows_in).astype(jnp.bfloat16)
        parts = [one_head(n, bits) for bits in range(mp_size)]
        a = jnp.concatenate([part[1] for part in parts], 1)
        g = jnp.concatenate([part[0] for part in parts], 1).astype(jnp.float32)
        gated = (norm_rows(a) * g).astype(jnp.bfloat16)
        y = jnp.dot(gated, wop[...], preferred_element_type=jnp.float32)
        y = jnp.where(positions < length, y + rows_in, 0.0).astype(jnp.bfloat16)
        for q in range(mp_size):
            send[s, q] = y[:, q * quarter : (q + 1) * quarter].reshape(MAXB, BLOCK, quarter)
        pick = jnp.where(picks == length - 1, 1.0, 0.0).astype(jnp.bfloat16)
        chosen = jnp.dot(pick, y, preferred_element_type=jnp.float32)
        for q in range(mp_size):
            state_out[s, q] = chosen[:, q * quarter : (q + 1) * quarter]
        pair = home * per_pair + j
        state_pair = there * per_pair + j
        for q in range(mp_size):
            own = jnp.logical_and(there == d, q == m)

            @pl.when(jnp.logical_not(own))
            def _():
                send_copy(s, q).start()

            @pl.when(own)
            def _():
                send_local(s, q, pair).start()

        for q in range(mp_size):
            own = jnp.logical_and(home == d, q == m)

            @pl.when(jnp.logical_not(own))
            def _():
                state_copy(s, q).start()

            @pl.when(own)
            def _():
                state_local(s, q, state_pair).start()

    def got_meta(step, carry):
        src = lax.rem(d + step, dp_size)
        pltpu.make_async_copy(meta_my.at[src], meta_in.at[src], meta_recv.at[src]).wait()
        return carry

    def read_meta():
        lax.fori_loop(1, dp_size, got_meta, 0)
        to_smem = pltpu.make_async_copy(meta_in, meta_s, local_sem)
        to_smem.start()
        to_smem.wait()

        def invert(i, row):
            src = i // per_pair
            j = i - src * per_pair
            length = meta_s[src, 0, 2 * j]
            offset = meta_s[src, 0, 2 * j + 1]
            for b in range(MAXB):
                at = jnp.where(length > b * BLOCK, offset + b, -1)
                row = jnp.where(lanes == at, MAXB * i + b, row)
            return row

        inv_v[...] = lax.fori_loop(
            0, pairs, invert, jnp.full((1, 128), zero_block, jnp.int32)
        )
        back = pltpu.make_async_copy(inv_v, inv_s, local_sem)
        back.start()
        back.wait()

    read_meta()

    def turn(i, carry):
        phase = i // slots
        s = i - phase * slots
        moved = moves(s)
        mine = jnp.where(moved, 2, jnp.where(crosses(s), 0, 1))

        @pl.when(mine == phase)
        def _():
            @pl.when(moved)
            def _():
                row_local(s).wait()

            k = s // per_pair
            j = s - k * per_pair
            src, _ = source(s)
            u, valid = user_of(target(s), j)
            home_len = jnp.where(valid, len_s[0, u], 0)
            one_user(s, jnp.where(moved, meta_s[src, 0, 2 * j], home_len))

        return carry

    lax.fori_loop(0, 3 * slots, turn, 0)

    def end_meta(step, carry):
        meta_copy(step).wait_send()
        return carry

    lax.fori_loop(1, dp_size, end_meta, 0)

    def end_rows(s, carry):
        @pl.when(moves(s))
        def _():
            row_copy(s).wait_send()

        return carry

    lax.fori_loop(0, slots, end_rows, 0)

    def sent(s, carry):
        _, home, there, _ = route(s)
        for q in range(mp_size):

            @pl.when(jnp.logical_not(jnp.logical_and(there == d, q == m)))
            def _():
                send_copy(s, q).wait_send()

            @pl.when(jnp.logical_not(jnp.logical_and(home == d, q == m)))
            def _():
                state_copy(s, q).wait_send()

        return carry

    lax.fori_loop(0, slots, sent, 0)

    def got(i, carry):
        send_local(0, 0, i).wait()
        state_local(0, 0, i).wait()
        return carry

    lax.fori_loop(0, pairs, got, 0)

    def place(b, carry):
        packed[b] = arr[inv_s[0, b]]
        return carry

    lax.fori_loop(0, blocks, place, 0)

    def pick_state(u, carry):
        at = owner_s[0, u] * per_pair + u // dp_size
        state32[pl.ds(u, 1), :] = state_in[at, 0:1, :]
        return carry

    lax.fori_loop(0, user_count, pick_state, 0)
    state[...] = state32[...].astype(state.dtype)


def per_device(tokens, w_uvqk, w_out, hist_len, owner, recv_offset, block_start):
    dp_size = lax.axis_size("dp")
    mp_size = lax.axis_size("mp")
    user_count = hist_len.shape[1]
    per_pair = -(-user_count // dp_size)
    pairs = dp_size * per_pair
    reach = dp_size // mp_size
    slots = reach * per_pair
    quarter = D // mp_size
    rows = tokens.shape[0]
    blocks = rows // BLOCK

    vmem = pl.BlockSpec(memory_space=pltpu.VMEM)
    anywhere = pl.BlockSpec(memory_space=pltpu.HBM)
    bf16, f32, i32 = jnp.bfloat16, jnp.float32, jnp.int32
    dma = pltpu.SemaphoreType.DMA
    packed, state = pl.pallas_call(
        functools.partial(layer_kernel, dp_size, mp_size, per_pair, user_count),
        out_shape=(
            jax.ShapeDtypeStruct((blocks, BLOCK, quarter), bf16),
            jax.ShapeDtypeStruct((user_count, quarter), bf16),
        ),
        in_specs=[anywhere] * 7,
        out_specs=(vmem, vmem),
        scratch_shapes=[
            pltpu.VMEM((blocks, BLOCK, D), bf16),
            pltpu.VMEM((2, slots, MAXB, BLOCK, D), bf16),
            pltpu.VMEM((mp_size, D, 4 * HEAD), bf16),
            pltpu.VMEM((D, D), bf16),
            pltpu.VMEM((slots, mp_size, MAXB, BLOCK, quarter), bf16),
            pltpu.VMEM((slots, mp_size, 8, quarter), f32),
            pltpu.VMEM((MAXB * pairs + 1, BLOCK, quarter), bf16),
            pltpu.VMEM((pairs, 8, quarter), f32),
            pltpu.VMEM((user_count, quarter), f32),
            pltpu.VMEM((dp_size, 1, 128), i32),
            pltpu.VMEM((dp_size, 1, 128), i32),
            pltpu.VMEM((1, 128), i32),
            pltpu.SMEM((1, user_count), i32),
            pltpu.SMEM((1, user_count), i32),
            pltpu.SMEM((1, user_count), i32),
            pltpu.SMEM((1, user_count), i32),
            pltpu.SMEM((dp_size, 1, 128), i32),
            pltpu.SMEM((1, 128), i32),
            dma((4,)),
            dma,
            dma,
            dma((mp_size,)),
            dma((3, CHUNKS)),
            dma((3, CHUNKS)),
            dma((dp_size,)),
            dma((dp_size,)),
            dma((slots,)),
            dma((slots,)),
            dma((slots, mp_size)),
            dma((pairs,)),
            dma((slots, mp_size)),
            dma((pairs,)),
            dma,
        ],
        compiler_params=pltpu.CompilerParams(
            collective_id=0, has_side_effects=True, vmem_limit_bytes=48 * 1024 * 1024
        ),
        name="layer",
    )(
        tokens.reshape(blocks, BLOCK, D), w_uvqk, w_out, owner, hist_len, recv_offset, block_start
    )
    return packed.reshape(rows, quarter), state


def solution(mesh):
    in_specs = (
        P("dp", None),
        P(None, "mp"),
        P(),
        P("dp", None),
        P("dp", None),
        P("dp", None),
        P("dp", None),
    )
    out_specs = (P("dp", "mp"), P("dp", "mp"))
    return jax.shard_map(
        per_device, mesh=mesh, in_specs=in_specs, out_specs=out_specs, check_vma=False
    )
```

time: 63.5 us -> 57.7 us (0.909)
  Pallas kernels: 62.1 us -> 49.6 us
  local copies, waits for them, and re-layouts: 0 us -> 6.43 us
    pallas_call x2 -> x0, Pallas kernels: 8.42 us -> none  [the longest x1 4.46 us: per_device(): pl.pallas_call(functools.partial(place_kernel, dp_size, per_pair), out_sh...]
    unnamed x0 -> x14, local copies, waits for them, and re-layouts: none -> 6.43 us
    pallas_call x1, Pallas kernels: 53.7 us -> 49.6 us  [per_device(): pl.pallas_call(functools.partial(layer_kernel, dp_size, mp_size, per_pair...]
where the time goes in v1:
time: 57.7 us; the launch traced here: 56.7 us
  Pallas kernels  49.6 us (86%)
  local copies, waits for them, and re-layouts  6.43 us (11%)
  between operations  0.65 us (1%)
    pallas_call x1, Pallas kernels, per_device(): pl.pallas_call(functools.partial(layer_kernel, dp_size, mp_size, per_pair...  49.6 us
    unnamed x14, local copies, waits for them, and re-layouts  6.43 us

profile of v1, /device:TPU:1, one launch (start us, length us, event | category | flops | bytes accessed | tf_op | source)
XLA Modules:
  0.0 56.7 jit_solution(17958209254500188094)
XLA Ops:
  0.6 0.0 copy-start
  0.6 1.0 %copy-done = bf16[512,512]{1,0:T(8,128)(2,1)S(1)} copy-done((bf16[512,512]{1,0:T(8,128)(2,1)S(1)}, bf16[512,512]{1,0:T(8,128)(2,1)}, u32[]{:S(2)}) %copy-start) | copy-done | bytes 524312
  1.7 0.0 copy-start.1
  1.7 1.0 %copy-done.1 = bf16[512,512]{1,0:T(8,128)(2,1)S(1)} copy-done((bf16[512,512]{1,0:T(8,128)(2,1)S(1)}, bf16[512,512]{1,0:T(8,128)(2,1)}, u32[]{:S(2)}) %copy-start.1) | copy-done | bytes 524312
  2.7 0.0 copy-start.2
  2.7 0.7 %copy-done.2 = s32[1,24]{1,0:T(1,128)S(1)} copy-done((s32[1,24]{1,0:T(1,128)S(1)}, s32[1,24]{1,0:T(1,128)}, u32[]{:S(2)}) %copy-start.2) | copy-done | bytes 120
  3.4 0.0 copy-start.3
  3.4 0.7 %copy-done.3 = s32[1,24]{1,0:T(1,128)S(1)} copy-done((s32[1,24]{1,0:T(1,128)S(1)}, s32[1,24]{1,0:T(1,128)}, u32[]{:S(2)}) %copy-start.3) | copy-done | bytes 120
  4.0 0.0 copy-start.4
  4.0 0.7 %copy-done.4 = s32[1,24]{1,0:T(1,128)S(1)} copy-done((s32[1,24]{1,0:T(1,128)S(1)}, s32[1,24]{1,0:T(1,128)}, u32[]{:S(2)}) %copy-start.4) | copy-done | bytes 120
  4.7 0.0 copy-start.5
  4.7 0.7 %copy-done.5 = s32[1,24]{1,0:T(1,128)S(1)} copy-done((s32[1,24]{1,0:T(1,128)S(1)}, s32[1,24]{1,0:T(1,128)}, u32[]{:S(2)}) %copy-start.5) | copy-done | bytes 120
  5.3 49.6 %layer.1 = (bf16[48,128,128]{2,1,0:T(8,128)(2,1)S(1)}, bf16[24,128]{1,0:T(8,128)(2,1)S(1)}) custom-call(bf16[48,128,512]{2,1,0:T(8,128)(2,1)} %bitcast.3, bf16[512,512]{1,0:T(8,128)(2,1)S(1)} %copy-done, bf16[512,512]{1,0:T(8,128)(2,1)S(1)} %copy-done.1, s32[1,24]{1,0:T(1,128)S(1)} %copy-done.2, s32[1,24]{1,0:T(1,128)S(1)} %copy-done.3, ...), custom_call_target="tpu_custom_call" | custom-call | tf_op jit(solution)/shard_map/layer/pallas_call | solution.py:448
  55.0 1.1 %copy.11 = bf16[6144,128]{1,0:T(8,128)(2,1)} copy(bf16[6144,128]{1,0:T(8,128)(2,1)S(1)} %bitcast.2) | data formatting | bytes 3145728
  56.1 0.6 %copy.12 = bf16[24,128]{1,0:T(8,128)(2,1)} copy(bf16[24,128]{1,0:T(8,128)(2,1)S(1)} %get-tuple-element.9) | data formatting | bytes 12288
Async XLA Ops:
  0.6 1.0 %copy-start = (bf16[512,512]{1,0:T(8,128)(2,1)S(1)}, bf16[512,512]{1,0:T(8,128)(2,1)}, u32[]{:S(2)}) copy-start(bf16[512,512]{1,0:T(8,128)(2,1)} %w_hbm.1) | copy-start | bytes 1572868
  1.7 1.0 %copy-start.1 = (bf16[512,512]{1,0:T(8,128)(2,1)S(1)}, bf16[512,512]{1,0:T(8,128)(2,1)}, u32[]{:S(2)}) copy-start(bf16[512,512]{1,0:T(8,128)(2,1)} %wout_hbm.1) | copy-start | bytes 1572868
  2.7 0.7 %copy-start.2 = (s32[1,24]{1,0:T(1,128)S(1)}, s32[1,24]{1,0:T(1,128)}, u32[]{:S(2)}) copy-start(s32[1,24]{1,0:T(1,128)} %owner_hbm.1) | copy-start | bytes 292
  3.4 0.7 %copy-start.3 = (s32[1,24]{1,0:T(1,128)S(1)}, s32[1,24]{1,0:T(1,128)}, u32[]{:S(2)}) copy-start(s32[1,24]{1,0:T(1,128)} %len_hbm.1) | copy-start | bytes 292
  4.0 0.7 %copy-start.4 = (s32[1,24]{1,0:T(1,128)S(1)}, s32[1,24]{1,0:T(1,128)}, u32[]{:S(2)}) copy-start(s32[1,24]{1,0:T(1,128)} %off_hbm.1) | copy-start | bytes 292
  4.7 0.7 %copy-start.5 = (s32[1,24]{1,0:T(1,128)S(1)}, s32[1,24]{1,0:T(1,128)}, u32[]{:S(2)}) copy-start(s32[1,24]{1,0:T(1,128)} %start_hbm.1) | copy-start | bytes 292

commit v2 on v1

--- a/solution.py
+++ b/solution.py
@@ -26,11 +26,11 @@
 
 def layer_kernel(
     dp_size, mp_size, per_pair, user_count,
-    tok_hbm, w_hbm, wout_hbm, owner_hbm, len_hbm, off_hbm, start_hbm,
+    tok_hbm, w_hbm, wout_hbm, owner_s, len_s, off_s, start_s,
     packed, state,
     tok, buf, wg, wop, send, state_out, arr, state_in, state32, meta_my, meta_in, inv_v,
-    owner_s, len_s, off_s, start_s, meta_s, inv_s,
-    tab_sem, tok_sem, w_sem, wop_sem, w_send, w_recv, meta_send, meta_recv, row_send, row_recv,
+    meta_s, inv_s,
+    tok_sem, w_sem, wop_sem, w_send, w_recv, meta_send, meta_recv, row_send, row_recv,
     send_sem, recv_sem, state_send, state_recv, local_sem,
 ):
     d = lax.axis_index("dp")
@@ -49,14 +49,6 @@
         pl.semaphore_signal(barrier, inc=1, device_id={"dp": o, "mp": q}, device_id_type=MESH)
         return carry
 
-    tables = [
-        pltpu.make_async_copy(src, dst, tab_sem.at[i])
-        for i, (src, dst) in enumerate(
-            ((owner_hbm, owner_s), (len_hbm, len_s), (off_hbm, off_s), (start_hbm, start_s))
-        )
-    ]
-    for table in tables:
-        table.start()
     tok_copy = pltpu.make_async_copy(tok_hbm, tok, tok_sem)
     tok_copy.start()
     own_w = pltpu.make_async_copy(w_hbm, wg.at[0], w_sem)
@@ -112,9 +104,6 @@
         u = first + j * dp_size
         valid = jnp.logical_and(found == 1, u < user_count)
         return jnp.minimum(u, user_count - 1), valid
-
-    for table in tables:
-        table.wait()
 
     lanes = lax.broadcasted_iota(jnp.int32, (1, 128), 1)
 
@@ -442,16 +431,17 @@
     blocks = rows // BLOCK
 
     vmem = pl.BlockSpec(memory_space=pltpu.VMEM)
+    smem = pl.BlockSpec(memory_space=pltpu.SMEM)
     anywhere = pl.BlockSpec(memory_space=pltpu.HBM)
     bf16, f32, i32 = jnp.bfloat16, jnp.float32, jnp.int32
     dma = pltpu.SemaphoreType.DMA
     packed, state = pl.pallas_call(
         functools.partial(layer_kernel, dp_size, mp_size, per_pair, user_count),
         out_shape=(
-            jax.ShapeDtypeStruct((blocks, BLOCK, quarter), bf16),
-            jax.ShapeDtypeStruct((user_count, quarter), bf16),
+            pltpu.VMEM((blocks, BLOCK, quarter), bf16),
+            pltpu.VMEM((user_count, quarter), bf16),
         ),
-        in_specs=[anywhere] * 7,
+        in_specs=[anywhere] * 3 + [smem] * 4,
         out_specs=(vmem, vmem),
         scratch_shapes=[
             pltpu.VMEM((blocks, BLOCK, D), bf16),
@@ -466,13 +456,8 @@
             pltpu.VMEM((dp_size, 1, 128), i32),
             pltpu.VMEM((dp_size, 1, 128), i32),
             pltpu.VMEM((1, 128), i32),
-            pltpu.SMEM((1, user_count), i32),
-            pltpu.SMEM((1, user_count), i32),
-            pltpu.SMEM((1, user_count), i32),
-            pltpu.SMEM((1, user_count), i32),
             pltpu.SMEM((dp_size, 1, 128), i32),
             pltpu.SMEM((1, 128), i32),
-            dma((4,)),
             dma,
             dma,
             dma((mp_size,)),
@@ -489,11 +474,15 @@
             dma,
         ],
         compiler_params=pltpu.CompilerParams(
-            collective_id=0, has_side_effects=True, vmem_limit_bytes=48 * 1024 * 1024
+            collective_id=0, has_side_effects=True, vmem_limit_bytes=56 * 1024 * 1024
         ),
         name="layer",
     )(
-        tokens.reshape(blocks, BLOCK, D), w_uvqk, w_out, owner, hist_len, recv_offset, block_start
+        *(
+            pltpu.with_memory_space_constraint(a, pltpu.HBM)
+            for a in (tokens.reshape(blocks, BLOCK, D), w_uvqk, w_out)
+        ),
+        owner, hist_len, recv_offset, block_start,
     )
     return packed.reshape(rows, quarter), state
 

time: 57.7 us -> 53.4 us (0.925)
  local copies, waits for them, and re-layouts: 6.43 us -> 1.74 us
  Pallas kernels: 49.6 us -> 50.3 us
    unnamed x14 -> x2, local copies, waits for them, and re-layouts: 6.43 us -> 1.74 us
    pallas_call x1, Pallas kernels: 49.6 us -> 50.3 us  [per_device(): pl.pallas_call(functools.partial(layer_kernel, dp_size, mp_size, per_pair...]
where the time goes in v2:
time: 53.4 us; the launch traced here: 52.7 us
  Pallas kernels  50.3 us (94%)
  local copies, waits for them, and re-layouts  1.74 us (3%)
  between operations  0.64 us (1%)
    pallas_call x1, Pallas kernels, per_device(): pl.pallas_call(functools.partial(layer_kernel, dp_size, mp_size, per_pair...  50.3 us
    unnamed x2, local copies, waits for them, and re-layouts  1.74 us

profile of v2, /device:TPU:1, one launch (start us, length us, event | category | flops | bytes accessed | tf_op | source)
XLA Modules:
  0.0 52.7 jit_solution(10663202086331563211)
XLA Ops:
  0.6 50.3 %layer.1 = (bf16[48,128,128]{2,1,0:T(8,128)(2,1)S(1)}, bf16[24,128]{1,0:T(8,128)(2,1)S(1)}) custom-call(bf16[48,128,512]{2,1,0:T(8,128)(2,1)} %bitcast.3, bf16[512,512]{1,0:T(8,128)(2,1)} %w_hbm.1, bf16[512,512]{1,0:T(8,128)(2,1)} %wout_hbm.1, s32[1,24]{1,0:T(1,128)} %owner_s.1, s32[1,24]{1,0:T(1,128)} %len_s.1, s32[1,24]{1,0:T(1,128)} %off_s.1, s32[1,24]{1,0:T(1,128)} %start_s.1), custom_call_target="tpu_custom_call" | custom-call | tf_op jit(solution)/shard_map/layer/pallas_call | solution.py:438
  50.9 1.1 %copy.11 = bf16[6144,128]{1,0:T(8,128)(2,1)} copy(bf16[6144,128]{1,0:T(8,128)(2,1)S(1)} %bitcast.2) | data formatting | bytes 3145728
  52.1 0.6 %copy.12 = bf16[24,128]{1,0:T(8,128)(2,1)} copy(bf16[24,128]{1,0:T(8,128)(2,1)S(1)} %get-tuple-element.7) | data formatting | bytes 12288

commit v3 on v1

v3 whole, which is shorter than its diff:
```python
import functools

import jax
import jax.numpy as jnp
from jax import lax
from jax.experimental import pallas as pl
from jax.experimental.pallas import tpu as pltpu
from jax.sharding import PartitionSpec as P

D = 512
HEADS = 4
HEAD = D // HEADS
BLOCK = 128
MAXB = 2
WIN = MAXB * BLOCK
EPS = 1e-05
CHUNKS = 4
MESH = pl.DeviceIdType.MESH


def norm_rows(values):
    average = jnp.mean(values, axis=-1, keepdims=True)
    variance = jnp.mean(values * values, axis=-1, keepdims=True) - average * average
    return (values - average) * lax.rsqrt(variance + EPS)


def layer_kernel(
    dp_size, mp_size, per_pair, moving, user_count,
    tok_hbm, w_hbm, wout_hbm, owner_hbm, len_hbm, off_hbm, start_hbm,
    arr, inv_s, state,
    tok, rows_out, rows_in, rows_home, wg, wop, wop_side, send, state_out, send_home, state_home,
    state_in, state32, meta_my, meta_in, inv_v, normed, gate, att,
    owner_s, len_s, off_s, start_s, meta_s,
    tab_sem, tok_sem, w_sem, wop_sem, side_sem, w_send, w_recv, meta_send, meta_recv, row_send, row_recv,
    send_sem, recv_sem, state_send, state_recv, send_home_sem, state_home_sem, local_sem,
):
    d = lax.axis_index("dp")
    m = lax.axis_index("mp")
    quarter = D // mp_size
    reach = dp_size // mp_size
    staying = per_pair - moving
    slots = reach * moving
    homes = 2 * reach * staying
    pairs = dp_size * per_pair
    side = D // 2
    first_q = m // 2 * 2
    last_block = tok_hbm.shape[0] - 1
    barrier = pltpu.get_barrier_semaphore()

    def greet(step, carry):
        o = lax.rem(d + step // mp_size, dp_size)
        q = lax.rem(m + lax.rem(step, mp_size), mp_size)
        pl.semaphore_signal(barrier, inc=1, device_id={"dp": o, "mp": q}, device_id_type=MESH)
        return carry

    lax.fori_loop(1, dp_size * mp_size, greet, 0)
    tables = [
        pltpu.make_async_copy(src, dst, tab_sem.at[i])
        for i, (src, dst) in enumerate(
            ((owner_hbm, owner_s), (start_hbm, start_s), (len_hbm, len_s), (off_hbm, off_s))
        )
    ]
    for table in tables:
        table.start()
    tok_copy = pltpu.make_async_copy(tok_hbm, tok, tok_sem)
    tok_copy.start()
    own_w = pltpu.make_async_copy(w_hbm, wg.at[0], w_sem)
    own_w.start()

    def flip(bits):
        if bits == 1:
            return m + 1 - 2 * lax.rem(m, 2)
        return lax.rem(m + 2, 4)

    wop_copies = []
    for bits in range(mp_size):
        head = m
        if bits & 1:
            head = head + 1 - 2 * lax.rem(head, 2)
        if bits & 2:
            head = lax.rem(head + 2, 4)
        copy = pltpu.make_async_copy(
            wout_hbm.at[pl.ds(pl.multiple_of(head * HEAD, HEAD), HEAD)],
            wop.at[pl.ds(bits * HEAD, HEAD)], wop_sem.at[bits],
        )
        copy.start()
        wop_copies.append(copy)
        if homes:
            copy = pltpu.make_async_copy(
                wout_hbm.at[
                    pl.ds(pl.multiple_of(head * HEAD, HEAD), HEAD),
                    pl.ds(pl.multiple_of(first_q * quarter, side), side),
                ],
                wop_side.at[pl.ds(bits * HEAD, HEAD)], side_sem.at[bits],
            )
            copy.start()
            wop_copies.append(copy)

    def target(s):
        k = s // moving
        return lax.rem(d + m + mp_size * k, dp_size), s - k * moving

    def source(s):
        k = s // moving
        return lax.rem(d - m - mp_size * k + 2 * dp_size, dp_size), s - k * moving

    def home_target(h):
        g = h // (reach * staying)
        r = h - g * (reach * staying)
        k = r // staying
        group = lax.rem(m + 2 * g, mp_size)
        return lax.rem(d + group + mp_size * k, dp_size), moving + r - k * staying

    def crosses(o):
        return (o < dp_size // 2) != (d < dp_size // 2)

    def find(o):
        first = 0
        found = 0
        for u in range(min(dp_size, user_count)):
            hit = owner_s[0, u] == o
            first = jnp.where(hit, u, first)
            found = jnp.where(hit, 1, found)
        return first, found

    def user_of(o, j):
        first, found = find(o)
        u = first + j * dp_size
        valid = jnp.logical_and(found == 1, u < user_count)
        return jnp.minimum(u, user_count - 1), valid

    for table in tables:
        table.wait()

    lanes = lax.broadcasted_iota(jnp.int32, (1, 128), 1)

    def fill_meta(o, carry):
        first, found = find(o)
        row = jnp.zeros((1, 128), jnp.int32)
        for j in range(per_pair):
            u = first + j * dp_size
            valid = jnp.logical_and(found == 1, u < user_count)
            u = jnp.minimum(u, user_count - 1)
            row = jnp.where(lanes == 2 * j, jnp.where(valid, len_s[0, u], 0), row)
            row = jnp.where(lanes == 2 * j + 1, off_s[0, u], row)
        meta_my[o] = row
        return carry

    lax.fori_loop(0, dp_size, fill_meta, 0)
    meta_in[d] = meta_my[d]
    zero_block = 2 * pairs
    arr[zero_block] = jnp.zeros((BLOCK, quarter), arr.dtype)
    tok_copy.wait()

    def stage(o, j, into):
        u, _ = user_of(o, j)
        start = start_s[0, u]
        for b in range(MAXB):
            into[b] = tok[jnp.minimum(start + b, last_block)]

    def stage_moved(s, carry):
        o, j = target(s)
        stage(o, j, rows_out.at[s])
        return carry

    def stage_home(h, carry):
        o, j = home_target(h)
        stage(o, j, rows_home.at[h])
        return carry

    lax.fori_loop(0, slots, stage_moved, 0)
    own_w.wait()

    pl.semaphore_wait(barrier, dp_size * mp_size - 1)

    def meta_copy(step):
        o = lax.rem(d + step, dp_size)
        return pltpu.make_async_remote_copy(
            src_ref=meta_my.at[o], dst_ref=meta_in.at[d], send_sem=meta_send.at[step],
            recv_sem=meta_recv.at[d], device_id={"dp": o}, device_id_type=MESH,
        )

    def start_meta(step, carry):
        meta_copy(step).start()
        return carry

    lax.fori_loop(1, dp_size, start_meta, 0)

    def row_copy(s):
        return pltpu.make_async_remote_copy(
            src_ref=rows_out.at[s], dst_ref=rows_in.at[s], send_sem=row_send.at[s],
            recv_sem=row_recv.at[s], device_id={"dp": target(s)[0]}, device_id_type=MESH,
        )

    def row_local(s):
        return pltpu.make_async_copy(rows_out.at[s], rows_in.at[s], row_recv.at[s])

    def start_rows(i, carry):
        late = i // slots
        s = i - late * slots
        o, _ = target(s)
        now = crosses(o) == (late == 0)

        @pl.when(jnp.logical_and(now, o != d))
        def _():
            row_copy(s).start()

        @pl.when(jnp.logical_and(now, o == d))
        def _():
            row_local(s).start()

        return carry

    lax.fori_loop(0, 2 * slots, start_rows, 0)

    piece = D // CHUNKS

    def w_copy(src, dst, chunk, peer, index):
        rows = pl.ds(chunk * piece, piece)
        return pltpu.make_async_remote_copy(
            src_ref=wg.at[src, rows], dst_ref=wg.at[dst, rows], send_sem=w_send.at[index, chunk],
            recv_sem=w_recv.at[index, chunk], device_id={"mp": peer}, device_id_type=MESH,
        )

    far = [w_copy(0, 2, c, flip(2), 1) for c in range(CHUNKS)]
    near = [w_copy(0, 1, c, flip(1), 0) for c in range(CHUNKS)]
    relay = [w_copy(2, 3, c, flip(1), 2) for c in range(CHUNKS)]
    for copy in far:
        copy.start()
    for copy in near:
        copy.start()

    lax.fori_loop(0, homes, stage_home, 0)

    causal = lax.broadcasted_iota(jnp.int32, (BLOCK, BLOCK), 1) <= lax.broadcasted_iota(
        jnp.int32, (BLOCK, BLOCK), 0
    )
    half_scale = 0.5 * HEAD ** (-0.5)

    def scores(q, k):
        t = lax.dot_general(
            q, k, (((1,), (1,)), ((), ())), preferred_element_type=jnp.float32
        ) * half_scale
        return t + t * jnp.tanh(t)

    def one_head(rows_in, bits):
        h = jnp.dot(rows_in, wg[bits], preferred_element_type=jnp.float32) * 0.5
        p = (h + h * jnp.tanh(h)).astype(jnp.bfloat16)
        u, v, q, k = (p[:, i * HEAD : (i + 1) * HEAD] for i in range(4))
        low = jnp.where(causal, scores(q[:BLOCK], k[:BLOCK]), 0.0).astype(jnp.bfloat16)
        back = scores(q[BLOCK:], k[:BLOCK])
        diag = jnp.where(causal, scores(q[BLOCK:], k[BLOCK:]), 0.0)
        high = jnp.concatenate([back, diag], 1).astype(jnp.bfloat16)
        first = jnp.dot(low, v[:BLOCK], preferred_element_type=jnp.float32)
        second = jnp.dot(high, v, preferred_element_type=jnp.float32)
        return u, jnp.concatenate([first, second], 0) * (1.0 / WIN)

    def send_copy(s, q):
        src, j = source(s)
        pair = src * per_pair + j
        return pltpu.make_async_remote_copy(
            src_ref=send.at[s, q], dst_ref=arr.at[pl.ds(MAXB * pair, MAXB)],
            send_sem=send_sem.at[s, q], recv_sem=recv_sem.at[pair],
            device_id={"mp": q}, device_id_type=MESH,
        )

    def send_local(s, q, pair):
        return pltpu.make_async_copy(
            send.at[s, q], arr.at[pl.ds(MAXB * pair, MAXB)], recv_sem.at[pair]
        )

    def state_copy(s, q):
        src, j = source(s)
        pair = d * per_pair + j
        return pltpu.make_async_remote_copy(
            src_ref=state_out.at[s, q], dst_ref=state_in.at[pair], send_sem=state_send.at[s, q],
            recv_sem=state_recv.at[pair], device_id={"dp": src, "mp": q}, device_id_type=MESH,
        )

    def state_local(s, q, pair):
        return pltpu.make_async_copy(state_out.at[s, q], state_in.at[pair], state_recv.at[pair])

    def home_copy(h, i):
        o, j = home_target(h)
        pair = d * per_pair + j
        return pltpu.make_async_remote_copy(
            src_ref=send_home.at[h, i], dst_ref=arr.at[pl.ds(MAXB * pair, MAXB)],
            send_sem=send_home_sem.at[h, i], recv_sem=recv_sem.at[pair],
            device_id={"dp": o, "mp": first_q + i}, device_id_type=MESH,
        )

    def home_local(h, i):
        pair = d * per_pair + home_target(h)[1]
        return pltpu.make_async_copy(
            send_home.at[h, i], arr.at[pl.ds(MAXB * pair, MAXB)], recv_sem.at[pair]
        )

    def home_state_copy(h, i):
        o, j = home_target(h)
        pair = o * per_pair + j
        return pltpu.make_async_remote_copy(
            src_ref=state_home.at[h, i], dst_ref=state_in.at[pair],
            send_sem=state_home_sem.at[h, i], recv_sem=state_recv.at[pair],
            device_id={"mp": first_q + i}, device_id_type=MESH,
        )

    def home_state_local(h, i):
        o, j = home_target(h)
        pair = o * per_pair + j
        return pltpu.make_async_copy(
            state_home.at[h, i], state_in.at[pair], state_recv.at[pair]
        )

    picks = lax.broadcasted_iota(jnp.int32, (8, WIN), 1)

    def finish(parts, x, weight, length, out, chosen):
        a = jnp.concatenate([part[1] for part in parts], 1)
        g = jnp.concatenate([part[0] for part in parts], 1).astype(jnp.float32)
        gated = (norm_rows(a) * g).astype(jnp.bfloat16)
        y = jnp.dot(gated, weight, preferred_element_type=jnp.float32)
        positions = lax.broadcasted_iota(jnp.int32, y.shape, 0)
        y = jnp.where(positions < length, y + x, 0.0).astype(jnp.bfloat16)
        pick = jnp.where(picks == length - 1, 1.0, 0.0).astype(jnp.bfloat16)
        row = jnp.dot(pick, y, preferred_element_type=jnp.float32)
        for i in range(y.shape[1] // quarter):
            out[i] = y[:, i * quarter : (i + 1) * quarter].reshape(MAXB, BLOCK, quarter)
            chosen[i] = row[:, i * quarter : (i + 1) * quarter]

    half = mp_size // 2

    def near_heads(h, carry):
        x = rows_home[h].reshape(WIN, D).astype(jnp.float32)
        n = norm_rows(x).astype(jnp.bfloat16)
        normed[h] = n
        parts = [one_head(n, bits) for bits in range(half)]
        gate[h] = jnp.concatenate([part[0] for part in parts], 1)
        att[h] = jnp.concatenate([part[1] for part in parts], 1)
        return carry

    def far_heads(i, carry):
        late = i // homes
        h = i - late * homes
        o, j = home_target(h)

        @pl.when(crosses(o) == (late == 0))
        def _():
            u, valid = user_of(o, j)
            length = jnp.where(valid, len_s[0, u], 0)
            n = normed[h]
            parts = [(gate[h], att[h])]
            parts += [one_head(n, bits) for bits in range(half, mp_size)]
            x = rows_home[h, :, :, pl.ds(pl.multiple_of(first_q * quarter, side), side)]
            x = x.reshape(WIN, side).astype(jnp.float32)
            finish(parts, x, wop_side[...], length, send_home.at[h], state_home.at[h])
            for i in range(2):
                @pl.when(first_q + i != m)
                def _():
                    home_state_copy(h, i).start()

                @pl.when(first_q + i == m)
                def _():
                    home_state_local(h, i).start()

            for i in range(2):
                own = jnp.logical_and(o == d, first_q + i == m)

                @pl.when(jnp.logical_not(own))
                def _():
                    home_copy(h, i).start()

                @pl.when(own)
                def _():
                    home_local(h, i).start()

        return carry

    def moved_user(i, carry):
        late = i // slots
        s = i - late * slots
        src, j = source(s)

        @pl.when(crosses(src) == (late == 1))
        def _():
            row_local(s).wait()
            x = rows_in[s].reshape(WIN, D).astype(jnp.float32)
            n = norm_rows(x).astype(jnp.bfloat16)
            parts = [one_head(n, bits) for bits in range(mp_size)]
            finish(parts, x, wop[...], meta_s[src, 0, 2 * j], send.at[s], state_out.at[s])
            for q in range(mp_size):
                own = jnp.logical_and(src == d, q == m)

                @pl.when(jnp.logical_not(own))
                def _():
                    state_copy(s, q).start()

                @pl.when(own)
                def _():
                    state_local(s, q, d * per_pair + j).start()

            for q in range(mp_size):
                @pl.when(q != m)
                def _():
                    send_copy(s, q).start()

                @pl.when(q == m)
                def _():
                    send_local(s, q, src * per_pair + j).start()

        return carry

    def got_meta(step, carry):
        src = lax.rem(d + step, dp_size)
        pltpu.make_async_copy(meta_my.at[src], meta_in.at[src], meta_recv.at[src]).wait()
        return carry

    def read_meta():
        lax.fori_loop(1, dp_size, got_meta, 0)
        to_smem = pltpu.make_async_copy(meta_in, meta_s, local_sem)
        to_smem.start()
        to_smem.wait()

        def invert(i, row):
            src = i // per_pair
            j = i - src * per_pair
            length = meta_s[src, 0, 2 * j]
            offset = meta_s[src, 0, 2 * j + 1]
            for b in range(MAXB):
                at = jnp.where(length > b * BLOCK, offset + b, -1)
                row = jnp.where(lanes == at, MAXB * i + b, row)
            return row

        inv_v[...] = lax.fori_loop(
            0, pairs, invert, jnp.full((1, 128), zero_block, jnp.int32)
        )
        back = pltpu.make_async_copy(inv_v, inv_s, local_sem)
        back.start()
        back.wait()

    for copy in near:
        copy.wait()
    if homes:
        lax.fori_loop(0, homes, near_heads, 0)
    for c in range(CHUNKS):
        far[c].wait()
        relay[c].start()
    read_meta()
    for copy in wop_copies:
        copy.wait()
    for c in range(CHUNKS):
        relay[c].wait()
    if homes:
        lax.fori_loop(0, 2 * homes, far_heads, 0)
    lax.fori_loop(0, 2 * slots, moved_user, 0)

    def end_meta(step, carry):
        meta_copy(step).wait_send()
        return carry

    lax.fori_loop(1, dp_size, end_meta, 0)

    def end_rows(s, carry):
        @pl.when(target(s)[0] != d)
        def _():
            row_copy(s).wait_send()

        return carry

    lax.fori_loop(0, slots, end_rows, 0)

    def sent(s, carry):
        src, _ = source(s)
        for q in range(mp_size):
            @pl.when(q != m)
            def _():
                send_copy(s, q).wait_send()

            @pl.when(jnp.logical_not(jnp.logical_and(src == d, q == m)))
            def _():
                state_copy(s, q).wait_send()

        return carry

    lax.fori_loop(0, slots, sent, 0)

    def home_sent(h, carry):
        o, _ = home_target(h)
        for i in range(2):
            @pl.when(first_q + i != m)
            def _():
                home_state_copy(h, i).wait_send()

            @pl.when(jnp.logical_not(jnp.logical_and(o == d, first_q + i == m)))
            def _():
                home_copy(h, i).wait_send()

        return carry

    if homes:
        lax.fori_loop(0, homes, home_sent, 0)

    def got_state(i, carry):
        state_local(0, 0, i).wait()
        return carry

    lax.fori_loop(0, pairs, got_state, 0)

    def pick_state(u, carry):
        at = owner_s[0, u] * per_pair + u // dp_size
        state32[pl.ds(u, 1), :] = state_in[at, 0:1, :]
        return carry

    lax.fori_loop(0, user_count, pick_state, 0)
    state[...] = state32[...].astype(state.dtype)

    def got(i, carry):
        send_local(0, 0, i).wait()
        return carry

    lax.fori_loop(0, pairs, got, 0)


def place_kernel(arr, inv, state_in, packed, state, out_sem, state_sem):
    blocks = packed.shape[0]

    def put(b, carry):
        pltpu.make_async_copy(arr.at[inv[0, b]], packed.at[b], out_sem).start()
        return carry

    lax.fori_loop(0, blocks, put, 0, unroll=8)
    out = pltpu.make_async_copy(state_in, state, state_sem)
    out.start()
    pltpu.make_async_copy(arr.at[pl.ds(0, blocks)], packed, out_sem).wait()
    out.wait()


def per_device(tokens, w_uvqk, w_out, hist_len, owner, recv_offset, block_start):
    dp_size = lax.axis_size("dp")
    mp_size = lax.axis_size("mp")
    user_count = hist_len.shape[1]
    per_pair = -(-user_count // dp_size)
    pairs = dp_size * per_pair
    reach = dp_size // mp_size
    moving = (2 * per_pair + 2) // 3
    slots = reach * moving
    homes = max(2 * reach * (per_pair - moving), 1)
    quarter = D // mp_size
    rows = tokens.shape[0]
    blocks = rows // BLOCK

    vmem = pl.BlockSpec(memory_space=pltpu.VMEM)
    smem = pl.BlockSpec(memory_space=pltpu.SMEM)
    anywhere = pl.BlockSpec(memory_space=pltpu.HBM)
    bf16, f32, i32 = jnp.bfloat16, jnp.float32, jnp.int32
    dma = pltpu.SemaphoreType.DMA
    arr, inv, state_rows = pl.pallas_call(
        functools.partial(layer_kernel, dp_size, mp_size, per_pair, moving, user_count),
        out_shape=(
            pltpu.VMEM((MAXB * pairs + 1, BLOCK, quarter), bf16),
            pltpu.SMEM((1, 128), i32),
            pltpu.VMEM((user_count, quarter), bf16),
        ),
        in_specs=[anywhere] * 7,
        out_specs=(vmem, smem, vmem),
        scratch_shapes=[
            pltpu.VMEM((blocks, BLOCK, D), bf16),
            pltpu.VMEM((slots, MAXB, BLOCK, D), bf16),
            pltpu.VMEM((slots, MAXB, BLOCK, D), bf16),
            pltpu.VMEM((homes, MAXB, BLOCK, D), bf16),
            pltpu.VMEM((mp_size, D, 4 * HEAD), bf16),
            pltpu.VMEM((D, D), bf16),
            pltpu.VMEM((D, D // 2), bf16),
            pltpu.VMEM((slots, mp_size, MAXB, BLOCK, quarter), bf16),
            pltpu.VMEM((slots, mp_size, 8, quarter), f32),
            pltpu.VMEM((homes, 2, MAXB, BLOCK, quarter), bf16),
            pltpu.VMEM((homes, 2, 8, quarter), f32),
            pltpu.VMEM((pairs, 8, quarter), f32),
            pltpu.VMEM((user_count, quarter), f32),
            pltpu.VMEM((dp_size, 1, 128), i32),
            pltpu.VMEM((dp_size, 1, 128), i32),
            pltpu.VMEM((1, 128), i32),
            pltpu.VMEM((homes, WIN, D), bf16),
            pltpu.VMEM((homes, WIN, D // 2), bf16),
            pltpu.VMEM((homes, WIN, D // 2), f32),
            pltpu.SMEM((1, user_count), i32),
            pltpu.SMEM((1, user_count), i32),
            pltpu.SMEM((1, user_count), i32),
            pltpu.SMEM((1, user_count), i32),
            pltpu.SMEM((dp_size, 1, 128), i32),
            dma((4,)),
            dma,
            dma,
            dma((mp_size,)),
            dma((mp_size,)),
            dma((3, CHUNKS)),
            dma((3, CHUNKS)),
            dma((dp_size,)),
            dma((dp_size,)),
            dma((slots,)),
            dma((slots,)),
            dma((slots, mp_size)),
            dma((pairs,)),
            dma((slots, mp_size)),
            dma((pairs,)),
            dma((homes, 2)),
            dma((homes, 2)),
            dma,
        ],
        compiler_params=pltpu.CompilerParams(
            collective_id=0, has_side_effects=True, vmem_limit_bytes=48 * 1024 * 1024
        ),
        name="layer",
    )(
        *(
            pltpu.with_memory_space_constraint(a, pltpu.HBM)
            for a in (
                tokens.reshape(blocks, BLOCK, D), w_uvqk, w_out,
                owner, hist_len, recv_offset, block_start,
            )
        )
    )
    packed, state = pl.pallas_call(
        place_kernel,
        out_shape=(
            jax.ShapeDtypeStruct((blocks, BLOCK, quarter), bf16),
            jax.ShapeDtypeStruct((user_count, quarter), bf16),
        ),
        in_specs=[vmem, smem, vmem],
        out_specs=(anywhere, anywhere),
        scratch_shapes=[dma, dma],
        compiler_params=pltpu.CompilerParams(vmem_limit_bytes=4 * 1024 * 1024),
        name="place",
    )(
        pltpu.with_memory_space_constraint(arr, pltpu.VMEM),
        pltpu.with_memory_space_constraint(inv, pltpu.SMEM),
        pltpu.with_memory_space_constraint(state_rows, pltpu.VMEM),
    )
    return packed.reshape(rows, quarter), state


def solution(mesh):
    in_specs = (
        P("dp", None),
        P(None, "mp"),
        P(),
        P("dp", None),
        P("dp", None),
        P("dp", None),
        P("dp", None),
    )
    out_specs = (P("dp", "mp"), P("dp", "mp"))
    return jax.shard_map(
        per_device, mesh=mesh, in_specs=in_specs, out_specs=out_specs, check_vma=False
    )
```

time: 57.7 us -> 48.2 us (0.84)
  local copies, waits for them, and re-layouts: 6.43 us -> 0 us
  Pallas kernels: 49.6 us -> 46.9 us
    unnamed x14 -> x0, local copies, waits for them, and re-layouts: 6.43 us -> none
    pallas_call x1, Pallas kernels: 49.6 us -> 45.8 us  [per_device(): pl.pallas_call(functools.partial(layer_kernel, dp_size, mp_size, per_pair...]
    pallas_call x0 -> x1, Pallas kernels: none -> 1.14 us  [per_device(): pl.pallas_call(place_kernel, out_shape=(jax.ShapeDtypeStruct((blocks, BLO...]
where the time goes in v3:
time: 48.2 us; the launch traced here: 47.6 us
  Pallas kernels  46.9 us (97%)
  between operations  0.64 us (1%)
    pallas_call x1, Pallas kernels, per_device(): pl.pallas_call(functools.partial(layer_kernel, dp_size, mp_size, per_pair...  45.8 us
    pallas_call x1, Pallas kernels, per_device(): pl.pallas_call(place_kernel, out_shape=(jax.ShapeDtypeStruct((blocks, BLO...  1.14 us

profile of v3, /device:TPU:1, one launch (start us, length us, event | category | flops | bytes accessed | tf_op | source)
XLA Modules:
  0.0 47.6 jit_solution(429483642441685315)
XLA Ops:
  0.6 45.8 %layer.1 = (bf16[49,128,128]{2,1,0:T(8,128)(2,1)S(1)}, s32[1,128]{1,0:T(1,128)S(4)}, bf16[24,128]{1,0:T(8,128)(2,1)S(1)}) custom-call(bf16[48,128,512]{2,1,0:T(8,128)(2,1)} %bitcast.2, bf16[512,512]{1,0:T(8,128)(2,1)} %w_hbm.1, bf16[512,512]{1,0:T(8,128)(2,1)} %wout_hbm.1, s32[1,24]{1,0:T(1,128)} %owner_hbm.1, s32[1,24]{1,0:T(1,128)} %len_hbm.1, ...), custom_call_target="tpu_custom_call" | custom-call | tf_op jit(solution)/shard_map/layer/pallas_call | solution.py:555
  46.5 1.1 %place.1 = (bf16[48,128,128]{2,1,0:T(8,128)(2,1)}, bf16[24,128]{1,0:T(8,128)(2,1)}) custom-call(bf16[49,128,128]{2,1,0:T(8,128)(2,1)S(1)} %get-tuple-element.7.arr, s32[1,128]{1,0:T(1,128)S(4)} %get-tuple-element.8.inv, bf16[24,128]{1,0:T(8,128)(2,1)S(1)} %get-tuple-element.9.state_in), custom_call_target="tpu_custom_call" | custom-call | tf_op jit(solution)/shard_map/place/pallas_call | solution.py:621

commit v4 on v3

--- a/solution.py
+++ b/solution.py
@@ -32,7 +32,7 @@
     state_in, state32, meta_my, meta_in, inv_v, normed, gate, att,
     owner_s, len_s, off_s, start_s, meta_s,
     tab_sem, tok_sem, w_sem, wop_sem, side_sem, w_send, w_recv, meta_send, meta_recv, row_send, row_recv,
-    send_sem, recv_sem, state_send, state_recv, send_home_sem, state_home_sem, local_sem,
+    send_sem, recv_sem, state_send, state_recv, send_home_sem, state_home_sem, local_sem, group_sem,
 ):
     d = lax.axis_index("dp")
     m = lax.axis_index("mp")
@@ -47,13 +47,17 @@
     last_block = tok_hbm.shape[0] - 1
     barrier = pltpu.get_barrier_semaphore()
 
-    def greet(step, carry):
-        o = lax.rem(d + step // mp_size, dp_size)
-        q = lax.rem(m + lax.rem(step, mp_size), mp_size)
-        pl.semaphore_signal(barrier, inc=1, device_id={"dp": o, "mp": q}, device_id_type=MESH)
-        return carry
-
-    lax.fori_loop(1, dp_size * mp_size, greet, 0)
+    tok_copy = pltpu.make_async_copy(tok_hbm, tok, tok_sem)
+    tok_copy.start()
+
+    for step in range(dp_size - 1, 0, -1):
+        pl.semaphore_signal(
+            barrier, inc=1, device_id={"dp": lax.rem(d + step, dp_size)}, device_id_type=MESH
+        )
+    for step in range(1, mp_size):
+        pl.semaphore_signal(
+            barrier, inc=1, device_id={"mp": lax.rem(m + step, mp_size)}, device_id_type=MESH
+        )
     tables = [
         pltpu.make_async_copy(src, dst, tab_sem.at[i])
         for i, (src, dst) in enumerate(
@@ -62,8 +66,6 @@
     ]
     for table in tables:
         table.start()
-    tok_copy = pltpu.make_async_copy(tok_hbm, tok, tok_sem)
-    tok_copy.start()
     own_w = pltpu.make_async_copy(w_hbm, wg.at[0], w_sem)
     own_w.start()
 
@@ -150,28 +152,23 @@
     meta_in[d] = meta_my[d]
     zero_block = 2 * pairs
     arr[zero_block] = jnp.zeros((BLOCK, quarter), arr.dtype)
-    tok_copy.wait()
-
     def stage(o, j, into):
         u, _ = user_of(o, j)
         start = start_s[0, u]
         for b in range(MAXB):
             into[b] = tok[jnp.minimum(start + b, last_block)]
 
-    def stage_moved(s, carry):
-        o, j = target(s)
-        stage(o, j, rows_out.at[s])
-        return carry
-
     def stage_home(h, carry):
         o, j = home_target(h)
         stage(o, j, rows_home.at[h])
         return carry
 
-    lax.fori_loop(0, slots, stage_moved, 0)
     own_w.wait()
-
-    pl.semaphore_wait(barrier, dp_size * mp_size - 1)
+    pl.semaphore_wait(barrier, dp_size + mp_size - 2)
+    for step in range(1, mp_size):
+        pl.semaphore_signal(
+            group_sem, inc=1, device_id={"mp": lax.rem(m + step, mp_size)}, device_id_type=MESH
+        )
 
     def meta_copy(step):
         o = lax.rem(d + step, dp_size)
@@ -194,24 +191,6 @@
 
     def row_local(s):
         return pltpu.make_async_copy(rows_out.at[s], rows_in.at[s], row_recv.at[s])
-
-    def start_rows(i, carry):
-        late = i // slots
-        s = i - late * slots
-        o, _ = target(s)
-        now = crosses(o) == (late == 0)
-
-        @pl.when(jnp.logical_and(now, o != d))
-        def _():
-            row_copy(s).start()
-
-        @pl.when(jnp.logical_and(now, o == d))
-        def _():
-            row_local(s).start()
-
-        return carry
-
-    lax.fori_loop(0, 2 * slots, start_rows, 0)
 
     piece = D // CHUNKS
 
@@ -230,6 +209,39 @@
     for copy in near:
         copy.start()
 
+    tok_copy.wait()
+
+    def stage_rows(i, carry):
+        late = i // slots
+        s = i - late * slots
+        o, j = target(s)
+
+        @pl.when(crosses(o) == (late == 0))
+        def _():
+            stage(o, j, rows_out.at[s])
+
+        return carry
+
+    def start_rows(i, carry):
+        late = i // slots
+        s = i - late * slots
+        o, _ = target(s)
+        now = crosses(o) == (late == 0)
+
+        @pl.when(jnp.logical_and(now, o != d))
+        def _():
+            row_copy(s).start()
+
+        @pl.when(jnp.logical_and(now, o == d))
+        def _():
+            row_local(s).start()
+
+        return carry
+
+    lax.fori_loop(0, slots, stage_rows, 0)
+    lax.fori_loop(0, slots, start_rows, 0)
+    lax.fori_loop(slots, 2 * slots, stage_rows, 0)
+    lax.fori_loop(slots, 2 * slots, start_rows, 0)
     lax.fori_loop(0, homes, stage_home, 0)
 
     causal = lax.broadcasted_iota(jnp.int32, (BLOCK, BLOCK), 1) <= lax.broadcasted_iota(
@@ -260,13 +272,13 @@
         pair = src * per_pair + j
         return pltpu.make_async_remote_copy(
             src_ref=send.at[s, q], dst_ref=arr.at[pl.ds(MAXB * pair, MAXB)],
-            send_sem=send_sem.at[s, q], recv_sem=recv_sem.at[pair],
+            send_sem=send_sem.at[s, q], recv_sem=recv_sem,
             device_id={"mp": q}, device_id_type=MESH,
         )
 
     def send_local(s, q, pair):
         return pltpu.make_async_copy(
-            send.at[s, q], arr.at[pl.ds(MAXB * pair, MAXB)], recv_sem.at[pair]
+            send.at[s, q], arr.at[pl.ds(MAXB * pair, MAXB)], recv_sem
         )
 
     def state_copy(s, q):
@@ -274,25 +286,25 @@
         pair = d * per_pair + j
         return pltpu.make_async_remote_copy(
             src_ref=state_out.at[s, q], dst_ref=state_in.at[pair], send_sem=state_send.at[s, q],
-            recv_sem=state_recv.at[pair], device_id={"dp": src, "mp": q}, device_id_type=MESH,
+            recv_sem=state_recv, device_id={"dp": src, "mp": q}, device_id_type=MESH,
         )
 
     def state_local(s, q, pair):
-        return pltpu.make_async_copy(state_out.at[s, q], state_in.at[pair], state_recv.at[pair])
+        return pltpu.make_async_copy(state_out.at[s, q], state_in.at[pair], state_recv)
 
     def home_copy(h, i):
         o, j = home_target(h)
         pair = d * per_pair + j
         return pltpu.make_async_remote_copy(
             src_ref=send_home.at[h, i], dst_ref=arr.at[pl.ds(MAXB * pair, MAXB)],
-            send_sem=send_home_sem.at[h, i], recv_sem=recv_sem.at[pair],
+            send_sem=send_home_sem.at[h, i], recv_sem=recv_sem,
             device_id={"dp": o, "mp": first_q + i}, device_id_type=MESH,
         )
 
     def home_local(h, i):
         pair = d * per_pair + home_target(h)[1]
         return pltpu.make_async_copy(
-            send_home.at[h, i], arr.at[pl.ds(MAXB * pair, MAXB)], recv_sem.at[pair]
+            send_home.at[h, i], arr.at[pl.ds(MAXB * pair, MAXB)], recv_sem
         )
 
     def home_state_copy(h, i):
@@ -300,7 +312,7 @@
         pair = o * per_pair + j
         return pltpu.make_async_remote_copy(
             src_ref=state_home.at[h, i], dst_ref=state_in.at[pair],
-            send_sem=state_home_sem.at[h, i], recv_sem=state_recv.at[pair],
+            send_sem=state_home_sem.at[h, i], recv_sem=state_recv,
             device_id={"mp": first_q + i}, device_id_type=MESH,
         )
 
@@ -308,7 +320,7 @@
         o, j = home_target(h)
         pair = o * per_pair + j
         return pltpu.make_async_copy(
-            state_home.at[h, i], state_in.at[pair], state_recv.at[pair]
+            state_home.at[h, i], state_in.at[pair], state_recv
         )
 
     picks = lax.broadcasted_iota(jnp.int32, (8, WIN), 1)
@@ -448,6 +460,7 @@
         copy.wait()
     for c in range(CHUNKS):
         relay[c].wait()
+    pl.semaphore_wait(group_sem, mp_size - 1)
     if homes:
         lax.fori_loop(0, 2 * homes, far_heads, 0)
     lax.fori_loop(0, 2 * slots, moved_user, 0)
@@ -498,11 +511,7 @@
     if homes:
         lax.fori_loop(0, homes, home_sent, 0)
 
-    def got_state(i, carry):
-        state_local(0, 0, i).wait()
-        return carry
-
-    lax.fori_loop(0, pairs, got_state, 0)
+    pltpu.make_async_copy(state_in, state_in, state_recv).wait()
 
     def pick_state(u, carry):
         at = owner_s[0, u] * per_pair + u // dp_size
@@ -512,11 +521,8 @@
     lax.fori_loop(0, user_count, pick_state, 0)
     state[...] = state32[...].astype(state.dtype)
 
-    def got(i, carry):
-        send_local(0, 0, i).wait()
-        return carry
-
-    lax.fori_loop(0, pairs, got, 0)
+    every = arr.at[pl.ds(0, MAXB * pairs)]
+    pltpu.make_async_copy(every, every, recv_sem).wait()
 
 
 def place_kernel(arr, inv, state_in, packed, state, out_sem, state_sem):
@@ -598,12 +604,13 @@
             dma((slots,)),
             dma((slots,)),
             dma((slots, mp_size)),
-            dma((pairs,)),
+            dma,
             dma((slots, mp_size)),
-            dma((pairs,)),
+            dma,
             dma((homes, 2)),
             dma((homes, 2)),
             dma,
+            pltpu.SemaphoreType.REGULAR,
         ],
         compiler_params=pltpu.CompilerParams(
             collective_id=0, has_side_effects=True, vmem_limit_bytes=48 * 1024 * 1024

time: 48.2 us -> 47.5 us (0.985)
  Pallas kernels: 46.9 us -> 46.3 us
    pallas_call x1, Pallas kernels: 45.8 us -> 45.2 us  [per_device(): pl.pallas_call(functools.partial(layer_kernel, dp_size, mp_size, per_pair...]
where the time goes in v4:
time: 47.5 us; the launch traced here: 47 us
  Pallas kernels  46.3 us (97%)
  between operations  0.64 us (1%)
    pallas_call x1, Pallas kernels, per_device(): pl.pallas_call(functools.partial(layer_kernel, dp_size, mp_size, per_pair...  45.2 us
    pallas_call x1, Pallas kernels, per_device(): pl.pallas_call(place_kernel, out_shape=(jax.ShapeDtypeStruct((blocks, BLO...  1.14 us

profile of v4, /device:TPU:1, one launch (start us, length us, event | category | flops | bytes accessed | tf_op | source)
XLA Modules:
  0.0 47.0 jit_solution(808457240809530021)
XLA Ops:
  0.6 45.2 %layer.1 = (bf16[49,128,128]{2,1,0:T(8,128)(2,1)S(1)}, s32[1,128]{1,0:T(1,128)S(4)}, bf16[24,128]{1,0:T(8,128)(2,1)S(1)}) custom-call(bf16[48,128,512]{2,1,0:T(8,128)(2,1)} %bitcast.2, bf16[512,512]{1,0:T(8,128)(2,1)} %w_hbm.1, bf16[512,512]{1,0:T(8,128)(2,1)} %wout_hbm.1, s32[1,24]{1,0:T(1,128)} %owner_hbm.1, s32[1,24]{1,0:T(1,128)} %len_hbm.1, ...), custom_call_target="tpu_custom_call" | custom-call | tf_op jit(solution)/shard_map/layer/pallas_call | solution.py:561
  45.8 1.1 %place.1 = (bf16[48,128,128]{2,1,0:T(8,128)(2,1)}, bf16[24,128]{1,0:T(8,128)(2,1)}) custom-call(bf16[49,128,128]{2,1,0:T(8,128)(2,1)S(1)} %get-tuple-element.7.arr, s32[1,128]{1,0:T(1,128)S(4)} %get-tuple-element.8.inv, bf16[24,128]{1,0:T(8,128)(2,1)S(1)} %get-tuple-element.9.state_in), custom_call_target="tpu_custom_call" | custom-call | tf_op jit(solution)/shard_map/place/pallas_call | solution.py:628

commit v5 on v4

--- a/solution.py
+++ b/solution.py
@@ -25,14 +25,15 @@
 
 
 def layer_kernel(
-    dp_size, mp_size, per_pair, moving, user_count,
+    dp_size, mp_size, per_pair, moving, user_count, bounds,
     tok_hbm, w_hbm, wout_hbm, owner_hbm, len_hbm, off_hbm, start_hbm,
     arr, inv_s, state,
-    tok, rows_out, rows_in, rows_home, wg, wop, wop_side, send, state_out, send_home, state_home,
+    parts_of_tok, rows_out, rows_in, rows_home, wg, wop, wop_side, send, state_out, send_home, state_home,
     state_in, state32, meta_my, meta_in, inv_v, normed, gate, att,
     owner_s, len_s, off_s, start_s, meta_s,
-    tab_sem, tok_sem, w_sem, wop_sem, side_sem, w_send, w_recv, meta_send, meta_recv, row_send, row_recv,
-    send_sem, recv_sem, state_send, state_recv, send_home_sem, state_home_sem, local_sem, group_sem,
+    tab_sem, tok_sem, w_sem, wop_sem, side_sem, w_send, w_recv, meta_send, meta_recv, fwd_send, fwd_recv,
+    row_send, row_recv,
+    send_sem, recv_sem, state_send, state_recv, send_home_sem, state_home_sem, local_sem, line_sem, group_sem,
 ):
     d = lax.axis_index("dp")
     m = lax.axis_index("mp")
@@ -44,16 +45,31 @@
     pairs = dp_size * per_pair
     side = D // 2
     first_q = m // 2 * 2
-    last_block = tok_hbm.shape[0] - 1
     barrier = pltpu.get_barrier_semaphore()
 
-    tok_copy = pltpu.make_async_copy(tok_hbm, tok, tok_sem)
-    tok_copy.start()
-
-    for step in range(dp_size - 1, 0, -1):
-        pl.semaphore_signal(
-            barrier, inc=1, device_id={"dp": lax.rem(d + step, dp_size)}, device_id_type=MESH
-        )
+    starts = (0,) + bounds[:-1]
+    tok_copies = [
+        pltpu.make_async_copy(
+            tok_hbm.at[pl.ds(starts[p], bounds[p] - starts[p])], part, tok_sem.at[p]
+        )
+        for p, part in enumerate(parts_of_tok)
+    ]
+    tok_copies[0].start()
+
+    def line_signal(semaphore):
+        def tell(k, carry):
+            ahead = m + mp_size * k
+            ahead = jnp.where(ahead == 0, mp_size, ahead)
+            for o in (d + ahead, d - ahead + dp_size):
+                pl.semaphore_signal(
+                    semaphore, inc=1, device_id={"dp": lax.rem(o, dp_size)}, device_id_type=MESH
+                )
+            return carry
+
+        lax.fori_loop(0, reach, tell, 0)
+
+    line_count = 2 * reach
+    line_signal(barrier)
     for step in range(1, mp_size):
         pl.semaphore_signal(
             barrier, inc=1, device_id={"mp": lax.rem(m + step, mp_size)}, device_id_type=MESH
@@ -67,7 +83,6 @@
     for table in tables:
         table.start()
     own_w = pltpu.make_async_copy(w_hbm, wg.at[0], w_sem)
-    own_w.start()
 
     def flip(bits):
         if bits == 1:
@@ -85,7 +100,6 @@
             wout_hbm.at[pl.ds(pl.multiple_of(head * HEAD, HEAD), HEAD)],
             wop.at[pl.ds(bits * HEAD, HEAD)], wop_sem.at[bits],
         )
-        copy.start()
         wop_copies.append(copy)
         if homes:
             copy = pltpu.make_async_copy(
@@ -95,7 +109,6 @@
                 ],
                 wop_side.at[pl.ds(bits * HEAD, HEAD)], side_sem.at[bits],
             )
-            copy.start()
             wop_copies.append(copy)
 
     def target(s):
@@ -136,7 +149,8 @@
 
     lanes = lax.broadcasted_iota(jnp.int32, (1, 128), 1)
 
-    def fill_meta(o, carry):
+    def fill_meta(k, carry):
+        o = lax.rem(d + m + mp_size * k, dp_size)
         first, found = find(o)
         row = jnp.zeros((1, 128), jnp.int32)
         for j in range(per_pair):
@@ -145,43 +159,67 @@
             u = jnp.minimum(u, user_count - 1)
             row = jnp.where(lanes == 2 * j, jnp.where(valid, len_s[0, u], 0), row)
             row = jnp.where(lanes == 2 * j + 1, off_s[0, u], row)
-        meta_my[o] = row
-        return carry
-
-    lax.fori_loop(0, dp_size, fill_meta, 0)
-    meta_in[d] = meta_my[d]
+        meta_my[k] = row
+
+        @pl.when(o == d)
+        def _():
+            meta_in[d] = row
+
+        return carry
+
+    lax.fori_loop(0, reach, fill_meta, 0)
     zero_block = 2 * pairs
     arr[zero_block] = jnp.zeros((BLOCK, quarter), arr.dtype)
     def stage(o, j, into):
         u, _ = user_of(o, j)
         start = start_s[0, u]
         for b in range(MAXB):
-            into[b] = tok[jnp.minimum(start + b, last_block)]
-
-    def stage_home(h, carry):
-        o, j = home_target(h)
-        stage(o, j, rows_home.at[h])
-        return carry
-
-    own_w.wait()
-    pl.semaphore_wait(barrier, dp_size + mp_size - 2)
-    for step in range(1, mp_size):
-        pl.semaphore_signal(
-            group_sem, inc=1, device_id={"mp": lax.rem(m + step, mp_size)}, device_id_type=MESH
-        )
-
-    def meta_copy(step):
-        o = lax.rem(d + step, dp_size)
+            at = jnp.minimum(start + b, bounds[j] - 1)
+            value = parts_of_tok[0][jnp.minimum(at, bounds[0] - 1)]
+            for p in range(1, j + 1):
+                other = parts_of_tok[p][jnp.clip(at - starts[p], 0, bounds[p] - starts[p] - 1)]
+                value = jnp.where(at >= starts[p], other, value)
+            into[b] = value
+
+    def stage_home(i, carry):
+        for j in range(moving, per_pair):
+            h = i * staying + j - moving
+            stage(home_target(h)[0], j, rows_home.at[h])
+        return carry
+
+    def meta_copy(k):
         return pltpu.make_async_remote_copy(
-            src_ref=meta_my.at[o], dst_ref=meta_in.at[d], send_sem=meta_send.at[step],
-            recv_sem=meta_recv.at[d], device_id={"dp": o}, device_id_type=MESH,
-        )
-
-    def start_meta(step, carry):
-        meta_copy(step).start()
-        return carry
-
-    lax.fori_loop(1, dp_size, start_meta, 0)
+            src_ref=meta_my.at[k], dst_ref=meta_in.at[d], send_sem=meta_send.at[k],
+            recv_sem=meta_recv.at[k], device_id={"dp": lax.rem(d + m + mp_size * k, dp_size)},
+            device_id_type=MESH,
+        )
+
+    def start_meta(k, carry):
+        @pl.when(m + k != 0)
+        def _():
+            meta_copy(k).start()
+
+        return carry
+
+    def meta_from(lane, k):
+        return lax.rem(d - lane - mp_size * k + 2 * dp_size, dp_size)
+
+    def forward(k, step):
+        row = meta_in.at[meta_from(m, k)]
+        return pltpu.make_async_remote_copy(
+            src_ref=row, dst_ref=row, send_sem=fwd_send.at[k, step],
+            recv_sem=fwd_recv.at[k, m], device_id={"mp": lax.rem(m + step, mp_size)},
+            device_id_type=MESH,
+        )
+
+    def forward_meta(k, carry):
+        @pl.when(m + k != 0)
+        def _():
+            pltpu.make_async_copy(meta_my.at[k], meta_my.at[k], meta_recv.at[k]).wait()
+
+        for step in range(1, mp_size):
+            forward(k, step).start()
+        return carry
 
     def row_copy(s):
         return pltpu.make_async_remote_copy(
@@ -204,45 +242,63 @@
     far = [w_copy(0, 2, c, flip(2), 1) for c in range(CHUNKS)]
     near = [w_copy(0, 1, c, flip(1), 0) for c in range(CHUNKS)]
     relay = [w_copy(2, 3, c, flip(1), 2) for c in range(CHUNKS)]
+
+    def stage_rows(i, carry, j):
+        late = i // reach
+        s = (i - late * reach) * moving + j
+        o, _ = target(s)
+
+        @pl.when(crosses(o) == (late == 0))
+        def _():
+            stage(o, j, rows_out.at[s])
+
+        return carry
+
+    def start_rows(i, carry, j):
+        late = i // reach
+        s = (i - late * reach) * moving + j
+        o, _ = target(s)
+        now = crosses(o) == (late == 0)
+
+        @pl.when(jnp.logical_and(now, o != d))
+        def _():
+            row_copy(s).start()
+
+        @pl.when(jnp.logical_and(now, o == d))
+        def _():
+            row_local(s).start()
+
+        return carry
+
+    tok_copies[0].wait()
+    for copy in tok_copies[1:]:
+        copy.start()
+    own_w.start()
+    lax.fori_loop(0, 2 * reach, functools.partial(stage_rows, j=0), 0)
+    pl.semaphore_wait(barrier, line_count + mp_size - 1)
+    lax.fori_loop(0, reach, start_meta, 0)
+    lax.fori_loop(0, 2 * reach, functools.partial(start_rows, j=0), 0)
+    line_signal(line_sem)
+    own_w.wait()
     for copy in far:
         copy.start()
     for copy in near:
         copy.start()
-
-    tok_copy.wait()
-
-    def stage_rows(i, carry):
-        late = i // slots
-        s = i - late * slots
-        o, j = target(s)
-
-        @pl.when(crosses(o) == (late == 0))
-        def _():
-            stage(o, j, rows_out.at[s])
-
-        return carry
-
-    def start_rows(i, carry):
-        late = i // slots
-        s = i - late * slots
-        o, _ = target(s)
-        now = crosses(o) == (late == 0)
-
-        @pl.when(jnp.logical_and(now, o != d))
-        def _():
-            row_copy(s).start()
-
-        @pl.when(jnp.logical_and(now, o == d))
-        def _():
-            row_local(s).start()
-
-        return carry
-
-    lax.fori_loop(0, slots, stage_rows, 0)
-    lax.fori_loop(0, slots, start_rows, 0)
-    lax.fori_loop(slots, 2 * slots, stage_rows, 0)
-    lax.fori_loop(slots, 2 * slots, start_rows, 0)
-    lax.fori_loop(0, homes, stage_home, 0)
+    for j in range(1, moving):
+        tok_copies[j].wait()
+        lax.fori_loop(0, 2 * reach, functools.partial(stage_rows, j=j), 0)
+        lax.fori_loop(0, 2 * reach, functools.partial(start_rows, j=j), 0)
+    for copy in tok_copies[max(moving, 1):]:
+        copy.wait()
+    for copy in wop_copies:
+        copy.start()
+    lax.fori_loop(0, 2 * reach, stage_home, 0)
+    pl.semaphore_wait(line_sem, line_count)
+    for step in range(1, mp_size):
+        pl.semaphore_signal(
+            group_sem, inc=1, device_id={"mp": lax.rem(m + step, mp_size)}, device_id_type=MESH
+        )
+    lax.fori_loop(0, reach, forward_meta, 0)
 
     causal = lax.broadcasted_iota(jnp.int32, (BLOCK, BLOCK), 1) <= lax.broadcasted_iota(
         jnp.int32, (BLOCK, BLOCK), 0
@@ -386,12 +442,16 @@
 
         return carry
 
-    def moved_user(i, carry):
-        late = i // slots
-        s = i - late * slots
-        src, j = source(s)
-
-        @pl.when(crosses(src) == (late == 1))
+    def outer(o):
+        return jnp.logical_or(4 * o < dp_size, 4 * o >= 3 * dp_size)
+
+    def moved_user(i, carry, turn):
+        j = i // reach
+        s = (i - j * reach) * moving + j
+        src, _ = source(s)
+        mine = jnp.where(crosses(src), jnp.where(outer(src), 0, 2), 1)
+
+        @pl.when(mine == turn)
         def _():
             row_local(s).wait()
             x = rows_in[s].reshape(WIN, D).astype(jnp.float32)
@@ -420,13 +480,18 @@
 
         return carry
 
-    def got_meta(step, carry):
-        src = lax.rem(d + step, dp_size)
-        pltpu.make_async_copy(meta_my.at[src], meta_in.at[src], meta_recv.at[src]).wait()
-        return carry
-
     def read_meta():
-        lax.fori_loop(1, dp_size, got_meta, 0)
+        def got_meta(i, carry):
+            k = i // mp_size
+            lane = i - k * mp_size
+
+            @pl.when(lane != m)
+            def _():
+                pltpu.make_async_copy(meta_my.at[k], meta_my.at[k], fwd_recv.at[k, lane]).wait()
+
+            return carry
+
+        lax.fori_loop(0, reach * mp_size, got_meta, 0)
         to_smem = pltpu.make_async_copy(meta_in, meta_s, local_sem)
         to_smem.start()
         to_smem.wait()
@@ -461,15 +526,22 @@
     for c in range(CHUNKS):
         relay[c].wait()
     pl.semaphore_wait(group_sem, mp_size - 1)
+    lax.fori_loop(0, slots, functools.partial(moved_user, turn=0), 0)
     if homes:
         lax.fori_loop(0, 2 * homes, far_heads, 0)
-    lax.fori_loop(0, 2 * slots, moved_user, 0)
-
-    def end_meta(step, carry):
-        meta_copy(step).wait_send()
-        return carry
-
-    lax.fori_loop(1, dp_size, end_meta, 0)
+    lax.fori_loop(0, slots, functools.partial(moved_user, turn=1), 0)
+    lax.fori_loop(0, slots, functools.partial(moved_user, turn=2), 0)
+
+    def end_meta(k, carry):
+        @pl.when(m + k != 0)
+        def _():
+            meta_copy(k).wait_send()
+
+        for step in range(1, mp_size):
+            forward(k, step).wait_send()
+        return carry
+
+    lax.fori_loop(0, reach, end_meta, 0)
 
     def end_rows(s, carry):
         @pl.when(target(s)[0] != d)
@@ -552,6 +624,10 @@
     quarter = D // mp_size
     rows = tokens.shape[0]
     blocks = rows // BLOCK
+    bounds = tuple(
+        blocks - max(0, user_count - (j + 1) * dp_size) for j in range(per_pair)
+    )
+    sizes = [b - a for a, b in zip((0,) + bounds[:-1], bounds)]
 
     vmem = pl.BlockSpec(memory_space=pltpu.VMEM)
     smem = pl.BlockSpec(memory_space=pltpu.SMEM)
@@ -559,7 +635,7 @@
     bf16, f32, i32 = jnp.bfloat16, jnp.float32, jnp.int32
     dma = pltpu.SemaphoreType.DMA
     arr, inv, state_rows = pl.pallas_call(
-        functools.partial(layer_kernel, dp_size, mp_size, per_pair, moving, user_count),
+        functools.partial(layer_kernel, dp_size, mp_size, per_pair, moving, user_count, bounds),
         out_shape=(
             pltpu.VMEM((MAXB * pairs + 1, BLOCK, quarter), bf16),
             pltpu.SMEM((1, 128), i32),
@@ -568,7 +644,7 @@
         in_specs=[anywhere] * 7,
         out_specs=(vmem, smem, vmem),
         scratch_shapes=[
-            pltpu.VMEM((blocks, BLOCK, D), bf16),
+            tuple(pltpu.VMEM((size, BLOCK, D), bf16) for size in sizes),
             pltpu.VMEM((slots, MAXB, BLOCK, D), bf16),
             pltpu.VMEM((slots, MAXB, BLOCK, D), bf16),
             pltpu.VMEM((homes, MAXB, BLOCK, D), bf16),
@@ -581,7 +657,7 @@
             pltpu.VMEM((homes, 2, 8, quarter), f32),
             pltpu.VMEM((pairs, 8, quarter), f32),
             pltpu.VMEM((user_count, quarter), f32),
-            pltpu.VMEM((dp_size, 1, 128), i32),
+            pltpu.VMEM((reach, 1, 128), i32),
             pltpu.VMEM((dp_size, 1, 128), i32),
             pltpu.VMEM((1, 128), i32),
             pltpu.VMEM((homes, WIN, D), bf16),
@@ -593,14 +669,16 @@
             pltpu.SMEM((1, user_count), i32),
             pltpu.SMEM((dp_size, 1, 128), i32),
             dma((4,)),
-            dma,
+            dma((per_pair,)),
             dma,
             dma((mp_size,)),
             dma((mp_size,)),
             dma((3, CHUNKS)),
             dma((3, CHUNKS)),
-            dma((dp_size,)),
-            dma((dp_size,)),
+            dma((reach,)),
+            dma((reach,)),
+            dma((reach, mp_size)),
+            dma((reach, mp_size)),
             dma((slots,)),
             dma((slots,)),
             dma((slots, mp_size)),
@@ -610,6 +688,7 @@
             dma((homes, 2)),
             dma((homes, 2)),
             dma,
+            pltpu.SemaphoreType.REGULAR,
             pltpu.SemaphoreType.REGULAR,
         ],
         compiler_params=pltpu.CompilerParams(

time: 47.5 us -> 46.7 us (0.983)
  no operation moved by 1% of the time
where the time goes in v5:
time: 46.7 us; the launch traced here: 46.6 us
  Pallas kernels  45.9 us (98%)
  between operations  0.64 us (1%)
    pallas_call x1, Pallas kernels, per_device(): pl.pallas_call(functools.partial(layer_kernel, dp_size, mp_size, per_pair...  44.8 us
    pallas_call x1, Pallas kernels, per_device(): pl.pallas_call(place_kernel, out_shape=(jax.ShapeDtypeStruct((blocks, BLO...  1.14 us

profile of v5, /device:TPU:1, one launch (start us, length us, event | category | flops | bytes accessed | tf_op | source)
XLA Modules:
  0.0 46.6 jit_solution(8721850034175058052)
XLA Ops:
  0.6 44.8 %layer.1 = (bf16[49,128,128]{2,1,0:T(8,128)(2,1)S(1)}, s32[1,128]{1,0:T(1,128)S(4)}, bf16[24,128]{1,0:T(8,128)(2,1)S(1)}) custom-call(bf16[48,128,512]{2,1,0:T(8,128)(2,1)} %bitcast.2, bf16[512,512]{1,0:T(8,128)(2,1)} %w_hbm.1, bf16[512,512]{1,0:T(8,128)(2,1)} %wout_hbm.1, s32[1,24]{1,0:T(1,128)} %owner_hbm.1, s32[1,24]{1,0:T(1,128)} %len_hbm.1, ...), custom_call_target="tpu_custom_call" | custom-call | tf_op jit(solution)/shard_map/layer/pallas_call | solution.py:637
  45.4 1.1 %place.1 = (bf16[48,128,128]{2,1,0:T(8,128)(2,1)}, bf16[24,128]{1,0:T(8,128)(2,1)}) custom-call(bf16[49,128,128]{2,1,0:T(8,128)(2,1)S(1)} %get-tuple-element.7.arr, s32[1,128]{1,0:T(1,128)S(4)} %get-tuple-element.8.inv, bf16[24,128]{1,0:T(8,128)(2,1)S(1)} %get-tuple-element.9.state_in), custom_call_target="tpu_custom_call" | custom-call | tf_op jit(solution)/shard_map/place/pallas_call | solution.py:707

commit v6 on v5

--- a/solution.py
+++ b/solution.py
@@ -311,17 +311,24 @@
         ) * half_scale
         return t + t * jnp.tanh(t)
 
-    def one_head(rows_in, bits):
-        h = jnp.dot(rows_in, wg[bits], preferred_element_type=jnp.float32) * 0.5
-        p = (h + h * jnp.tanh(h)).astype(jnp.bfloat16)
-        u, v, q, k = (p[:, i * HEAD : (i + 1) * HEAD] for i in range(4))
-        low = jnp.where(causal, scores(q[:BLOCK], k[:BLOCK]), 0.0).astype(jnp.bfloat16)
-        back = scores(q[BLOCK:], k[:BLOCK])
-        diag = jnp.where(causal, scores(q[BLOCK:], k[BLOCK:]), 0.0)
-        high = jnp.concatenate([back, diag], 1).astype(jnp.bfloat16)
-        first = jnp.dot(low, v[:BLOCK], preferred_element_type=jnp.float32)
-        second = jnp.dot(high, v, preferred_element_type=jnp.float32)
-        return u, jnp.concatenate([first, second], 0) * (1.0 / WIN)
+    def heads(n, which):
+        hidden = [jnp.dot(n, wg[bits], preferred_element_type=jnp.float32) for bits in which]
+        projected = [(h + h * jnp.tanh(h)).astype(jnp.bfloat16) for h in hidden]
+        weights = []
+        for p in projected:
+            q, k = p[:, 2 * HEAD : 3 * HEAD], p[:, 3 * HEAD :]
+            low = jnp.where(causal, scores(q[:BLOCK], k[:BLOCK]), 0.0)
+            high = scores(q[BLOCK:], k)
+            diag = jnp.where(causal, high[:, BLOCK:], 0.0)
+            high = jnp.concatenate([high[:, :BLOCK], diag], 1)
+            weights.append((low.astype(jnp.bfloat16), high.astype(jnp.bfloat16)))
+        parts = []
+        for p, (low, high) in zip(projected, weights):
+            v = p[:, HEAD : 2 * HEAD]
+            first = jnp.dot(low, v[:BLOCK], preferred_element_type=jnp.float32)
+            second = jnp.dot(high, v, preferred_element_type=jnp.float32)
+            parts.append((p[:, :HEAD], jnp.concatenate([first, second], 0) * (1.0 / WIN)))
+        return parts
 
     def send_copy(s, q):
         src, j = source(s)
@@ -398,9 +405,9 @@
 
     def near_heads(h, carry):
         x = rows_home[h].reshape(WIN, D).astype(jnp.float32)
-        n = norm_rows(x).astype(jnp.bfloat16)
+        n = (norm_rows(x) * 0.5).astype(jnp.bfloat16)
         normed[h] = n
-        parts = [one_head(n, bits) for bits in range(half)]
+        parts = heads(n, range(half))
         gate[h] = jnp.concatenate([part[0] for part in parts], 1)
         att[h] = jnp.concatenate([part[1] for part in parts], 1)
         return carry
@@ -416,7 +423,7 @@
             length = jnp.where(valid, len_s[0, u], 0)
             n = normed[h]
             parts = [(gate[h], att[h])]
-            parts += [one_head(n, bits) for bits in range(half, mp_size)]
+            parts += heads(n, range(half, mp_size))
             x = rows_home[h, :, :, pl.ds(pl.multiple_of(first_q * quarter, side), side)]
             x = x.reshape(WIN, side).astype(jnp.float32)
             finish(parts, x, wop_side[...], length, send_home.at[h], state_home.at[h])
@@ -455,8 +462,8 @@
         def _():
             row_local(s).wait()
             x = rows_in[s].reshape(WIN, D).astype(jnp.float32)
-            n = norm_rows(x).astype(jnp.bfloat16)
-            parts = [one_head(n, bits) for bits in range(mp_size)]
+            n = (norm_rows(x) * 0.5).astype(jnp.bfloat16)
+            parts = heads(n, range(mp_size))
             finish(parts, x, wop[...], meta_s[src, 0, 2 * j], send.at[s], state_out.at[s])
             for q in range(mp_size):
                 own = jnp.logical_and(src == d, q == m)

time: 46.7 us -> 44.5 us (0.953)
  Pallas kernels: 45.9 us -> 43.7 us
    pallas_call x1, Pallas kernels: 44.8 us -> 42.6 us  [per_device(): pl.pallas_call(functools.partial(layer_kernel, dp_size, mp_size, per_pair...]
where the time goes in v6:
time: 44.5 us; the launch traced here: 44.4 us
  Pallas kernels  43.7 us (98%)
  between operations  0.64 us (1%)
    pallas_call x1, Pallas kernels, per_device(): pl.pallas_call(functools.partial(layer_kernel, dp_size, mp_size, per_pair...  42.6 us
    pallas_call x1, Pallas kernels, per_device(): pl.pallas_call(place_kernel, out_shape=(jax.ShapeDtypeStruct((blocks, BLO...  1.14 us

profile of v6, /device:TPU:1, one launch (start us, length us, event | category | flops | bytes accessed | tf_op | source)
XLA Modules:
  0.0 44.4 jit_solution(6428832110130516864)
XLA Ops:
  0.6 42.6 %layer.1 = (bf16[49,128,128]{2,1,0:T(8,128)(2,1)S(1)}, s32[1,128]{1,0:T(1,128)S(4)}, bf16[24,128]{1,0:T(8,128)(2,1)S(1)}) custom-call(bf16[48,128,512]{2,1,0:T(8,128)(2,1)} %bitcast.2, bf16[512,512]{1,0:T(8,128)(2,1)} %w_hbm.1, bf16[512,512]{1,0:T(8,128)(2,1)} %wout_hbm.1, s32[1,24]{1,0:T(1,128)} %owner_hbm.1, s32[1,24]{1,0:T(1,128)} %len_hbm.1, ...), custom_call_target="tpu_custom_call" | custom-call | tf_op jit(solution)/shard_map/layer/pallas_call | solution.py:644
  43.2 1.1 %place.1 = (bf16[48,128,128]{2,1,0:T(8,128)(2,1)}, bf16[24,128]{1,0:T(8,128)(2,1)}) custom-call(bf16[49,128,128]{2,1,0:T(8,128)(2,1)S(1)} %get-tuple-element.7.arr, s32[1,128]{1,0:T(1,128)S(4)} %get-tuple-element.8.inv, bf16[24,128]{1,0:T(8,128)(2,1)S(1)} %get-tuple-element.9.state_in), custom_call_target="tpu_custom_call" | custom-call | tf_op jit(solution)/shard_map/place/pallas_call | solution.py:714

commit v7 on v6

--- a/solution.py
+++ b/solution.py
@@ -25,7 +25,7 @@
 
 
 def layer_kernel(
-    dp_size, mp_size, per_pair, moving, user_count, bounds,
+    dp_size, mp_size, per_pair, moving, inner_moving, user_count, bounds,
     tok_hbm, w_hbm, wout_hbm, owner_hbm, len_hbm, off_hbm, start_hbm,
     arr, inv_s, state,
     parts_of_tok, rows_out, rows_in, rows_home, wg, wop, wop_side, send, state_out, send_home, state_home,
@@ -39,7 +39,7 @@
     m = lax.axis_index("mp")
     quarter = D // mp_size
     reach = dp_size // mp_size
-    staying = per_pair - moving
+    staying = per_pair - inner_moving
     slots = reach * moving
     homes = 2 * reach * staying
     pairs = dp_size * per_pair
@@ -124,10 +124,22 @@
         r = h - g * (reach * staying)
         k = r // staying
         group = lax.rem(m + 2 * g, mp_size)
-        return lax.rem(d + group + mp_size * k, dp_size), moving + r - k * staying
+        return lax.rem(d + group + mp_size * k, dp_size), inner_moving + r - k * staying
 
     def crosses(o):
         return (o < dp_size // 2) != (d < dp_size // 2)
+
+    def outer(o):
+        return jnp.logical_or(4 * o < dp_size, 4 * o >= 3 * dp_size)
+
+    def moves(src, o, j):
+        few = jnp.logical_and(crosses(src + o - d), jnp.logical_not(outer(src)))
+        few = jnp.logical_and(few, lax.rem(m, 2) == 0)
+        return j < jnp.where(few, inner_moving, moving)
+
+    def stays(h):
+        o, j = home_target(h)
+        return jnp.logical_not(moves(d, o, j))
 
     def find(o):
         first = 0
@@ -182,9 +194,13 @@
             into[b] = value
 
     def stage_home(i, carry):
-        for j in range(moving, per_pair):
-            h = i * staying + j - moving
-            stage(home_target(h)[0], j, rows_home.at[h])
+        for j in range(inner_moving, per_pair):
+            h = i * staying + j - inner_moving
+
+            @pl.when(stays(h))
+            def _():
+                stage(home_target(h)[0], j, rows_home.at[h])
+
         return carry
 
     def meta_copy(k):
@@ -248,7 +264,7 @@
         s = (i - late * reach) * moving + j
         o, _ = target(s)
 
-        @pl.when(crosses(o) == (late == 0))
+        @pl.when(jnp.logical_and(crosses(o) == (late == 0), moves(d, o, j)))
         def _():
             stage(o, j, rows_out.at[s])
 
@@ -258,7 +274,7 @@
         late = i // reach
         s = (i - late * reach) * moving + j
         o, _ = target(s)
-        now = crosses(o) == (late == 0)
+        now = jnp.logical_and(crosses(o) == (late == 0), moves(d, o, j))
 
         @pl.when(jnp.logical_and(now, o != d))
         def _():
@@ -274,10 +290,12 @@
     for copy in tok_copies[1:]:
         copy.start()
     own_w.start()
-    lax.fori_loop(0, 2 * reach, functools.partial(stage_rows, j=0), 0)
     pl.semaphore_wait(barrier, line_count + mp_size - 1)
     lax.fori_loop(0, reach, start_meta, 0)
-    lax.fori_loop(0, 2 * reach, functools.partial(start_rows, j=0), 0)
+    lax.fori_loop(0, reach, functools.partial(stage_rows, j=0), 0)
+    lax.fori_loop(0, reach, functools.partial(start_rows, j=0), 0)
+    lax.fori_loop(reach, 2 * reach, functools.partial(stage_rows, j=0), 0)
+    lax.fori_loop(reach, 2 * reach, functools.partial(start_rows, j=0), 0)
     line_signal(line_sem)
     own_w.wait()
     for copy in far:
@@ -404,20 +422,26 @@
     half = mp_size // 2
 
     def near_heads(h, carry):
+        @pl.when(stays(h))
+        def _():
+            near_user(h)
+
+        return carry
+
+    def near_user(h):
         x = rows_home[h].reshape(WIN, D).astype(jnp.float32)
         n = (norm_rows(x) * 0.5).astype(jnp.bfloat16)
         normed[h] = n
         parts = heads(n, range(half))
         gate[h] = jnp.concatenate([part[0] for part in parts], 1)
         att[h] = jnp.concatenate([part[1] for part in parts], 1)
-        return carry
 
     def far_heads(i, carry):
         late = i // homes
         h = i - late * homes
         o, j = home_target(h)
 
-        @pl.when(crosses(o) == (late == 0))
+        @pl.when(jnp.logical_and(crosses(o) == (late == 0), stays(h)))
         def _():
             u, valid = user_of(o, j)
             length = jnp.where(valid, len_s[0, u], 0)
@@ -449,16 +473,13 @@
 
         return carry
 
-    def outer(o):
-        return jnp.logical_or(4 * o < dp_size, 4 * o >= 3 * dp_size)
-
     def moved_user(i, carry, turn):
         j = i // reach
         s = (i - j * reach) * moving + j
         src, _ = source(s)
         mine = jnp.where(crosses(src), jnp.where(outer(src), 0, 2), 1)
 
-        @pl.when(mine == turn)
+        @pl.when(jnp.logical_and(mine == turn, moves(src, d, j)))
         def _():
             row_local(s).wait()
             x = rows_in[s].reshape(WIN, D).astype(jnp.float32)
@@ -551,7 +572,9 @@
     lax.fori_loop(0, reach, end_meta, 0)
 
     def end_rows(s, carry):
-        @pl.when(target(s)[0] != d)
+        o, j = target(s)
+
+        @pl.when(jnp.logical_and(o != d, moves(d, o, j)))
         def _():
             row_copy(s).wait_send()
 
@@ -560,13 +583,14 @@
     lax.fori_loop(0, slots, end_rows, 0)
 
     def sent(s, carry):
-        src, _ = source(s)
+        src, j = source(s)
+        mine = moves(src, d, j)
         for q in range(mp_size):
-            @pl.when(q != m)
+            @pl.when(jnp.logical_and(q != m, mine))
             def _():
                 send_copy(s, q).wait_send()
 
-            @pl.when(jnp.logical_not(jnp.logical_and(src == d, q == m)))
+            @pl.when(jnp.logical_and(jnp.logical_not(jnp.logical_and(src == d, q == m)), mine))
             def _():
                 state_copy(s, q).wait_send()
 
@@ -576,12 +600,15 @@
 
     def home_sent(h, carry):
         o, _ = home_target(h)
+        mine = stays(h)
         for i in range(2):
-            @pl.when(first_q + i != m)
+            @pl.when(jnp.logical_and(first_q + i != m, mine))
             def _():
                 home_state_copy(h, i).wait_send()
 
-            @pl.when(jnp.logical_not(jnp.logical_and(o == d, first_q + i == m)))
+            @pl.when(
+                jnp.logical_and(jnp.logical_not(jnp.logical_and(o == d, first_q + i == m)), mine)
+            )
             def _():
                 home_copy(h, i).wait_send()
 
@@ -627,7 +654,8 @@
     reach = dp_size // mp_size
     moving = (2 * per_pair + 2) // 3
     slots = reach * moving
-    homes = max(2 * reach * (per_pair - moving), 1)
+    inner_moving = max(moving - 1, 1)
+    homes = max(2 * reach * (per_pair - inner_moving), 1)
     quarter = D // mp_size
     rows = tokens.shape[0]
     blocks = rows // BLOCK
@@ -642,7 +670,7 @@
     bf16, f32, i32 = jnp.bfloat16, jnp.float32, jnp.int32
     dma = pltpu.SemaphoreType.DMA
     arr, inv, state_rows = pl.pallas_call(
-        functools.partial(layer_kernel, dp_size, mp_size, per_pair, moving, user_count, bounds),
+        functools.partial(layer_kernel, dp_size, mp_size, per_pair, moving, inner_moving, user_count, bounds),
         out_shape=(
             pltpu.VMEM((MAXB * pairs + 1, BLOCK, quarter), bf16),
             pltpu.SMEM((1, 128), i32),

time: 44.5 us -> 44 us (0.989)
  Pallas kernels: 43.7 us -> 43 us
    pallas_call x1, Pallas kernels: 42.6 us -> 41.9 us  [per_device(): pl.pallas_call(functools.partial(layer_kernel, dp_size, mp_size, per_pair...]
where the time goes in v7:
time: 44 us; the launch traced here: 43.7 us
  Pallas kernels  43 us (98%)
  between operations  0.64 us (1%)
    pallas_call x1, Pallas kernels, per_device(): pl.pallas_call(functools.partial(layer_kernel, dp_size, mp_size, per_pair...  41.9 us
    pallas_call x1, Pallas kernels, per_device(): pl.pallas_call(place_kernel, out_shape=(jax.ShapeDtypeStruct((blocks, BLO...  1.14 us

profile of v7, /device:TPU:1, one launch (start us, length us, event | category | flops | bytes accessed | tf_op | source)
XLA Modules:
  0.0 43.7 jit_solution(10214354317809538925)
XLA Ops:
  0.6 41.9 %layer.1 = (bf16[49,128,128]{2,1,0:T(8,128)(2,1)S(1)}, s32[1,128]{1,0:T(1,128)S(4)}, bf16[24,128]{1,0:T(8,128)(2,1)S(1)}) custom-call(bf16[48,128,512]{2,1,0:T(8,128)(2,1)} %bitcast.2, bf16[512,512]{1,0:T(8,128)(2,1)} %w_hbm.1, bf16[512,512]{1,0:T(8,128)(2,1)} %wout_hbm.1, s32[1,24]{1,0:T(1,128)} %owner_hbm.1, s32[1,24]{1,0:T(1,128)} %len_hbm.1, ...), custom_call_target="tpu_custom_call" | custom-call | tf_op jit(solution)/shard_map/layer/pallas_call | solution.py:672
  42.5 1.1 %place.1 = (bf16[48,128,128]{2,1,0:T(8,128)(2,1)}, bf16[24,128]{1,0:T(8,128)(2,1)}) custom-call(bf16[49,128,128]{2,1,0:T(8,128)(2,1)S(1)} %get-tuple-element.7.arr, s32[1,128]{1,0:T(1,128)S(4)} %get-tuple-element.8.inv, bf16[24,128]{1,0:T(8,128)(2,1)S(1)} %get-tuple-element.9.state_in), custom_call_target="tpu_custom_call" | custom-call | tf_op jit(solution)/shard_map/place/pallas_call | solution.py:742

commit v8 on v7

--- a/solution.py
+++ b/solution.py
@@ -556,8 +556,10 @@
     pl.semaphore_wait(group_sem, mp_size - 1)
     lax.fori_loop(0, slots, functools.partial(moved_user, turn=0), 0)
     if homes:
-        lax.fori_loop(0, 2 * homes, far_heads, 0)
+        lax.fori_loop(0, homes, far_heads, 0)
     lax.fori_loop(0, slots, functools.partial(moved_user, turn=1), 0)
+    if homes:
+        lax.fori_loop(homes, 2 * homes, far_heads, 0)
     lax.fori_loop(0, slots, functools.partial(moved_user, turn=2), 0)
 
     def end_meta(k, carry):
@@ -638,9 +640,9 @@
         pltpu.make_async_copy(arr.at[inv[0, b]], packed.at[b], out_sem).start()
         return carry
 
-    lax.fori_loop(0, blocks, put, 0, unroll=8)
     out = pltpu.make_async_copy(state_in, state, state_sem)
     out.start()
+    lax.fori_loop(0, blocks, put, 0, unroll=True)
     pltpu.make_async_copy(arr.at[pl.ds(0, blocks)], packed, out_sem).wait()
     out.wait()
 

time: 44 us -> 44 us (level)
  no operation moved by 1% of the time
where the time goes in v8:
time: 44 us; the launch traced here: 43.7 us
  Pallas kernels  43 us (98%)
  between operations  0.64 us (1%)
    pallas_call x1, Pallas kernels, per_device(): pl.pallas_call(functools.partial(layer_kernel, dp_size, mp_size, per_pair...  41.9 us
    pallas_call x1, Pallas kernels, per_device(): pl.pallas_call(place_kernel, out_shape=(jax.ShapeDtypeStruct((blocks, BLO...  1.14 us

profile of v8, /device:TPU:1, one launch (start us, length us, event | category | flops | bytes accessed | tf_op | source)
XLA Modules:
  0.0 43.7 jit_solution(330552341797281525)
XLA Ops:
  0.6 41.9 %layer.1 = (bf16[49,128,128]{2,1,0:T(8,128)(2,1)S(1)}, s32[1,128]{1,0:T(1,128)S(4)}, bf16[24,128]{1,0:T(8,128)(2,1)S(1)}) custom-call(bf16[48,128,512]{2,1,0:T(8,128)(2,1)} %bitcast.2, bf16[512,512]{1,0:T(8,128)(2,1)} %w_hbm.1, bf16[512,512]{1,0:T(8,128)(2,1)} %wout_hbm.1, s32[1,24]{1,0:T(1,128)} %owner_hbm.1, s32[1,24]{1,0:T(1,128)} %len_hbm.1, ...), custom_call_target="tpu_custom_call" | custom-call | tf_op jit(solution)/shard_map/layer/pallas_call | solution.py:674
  42.5 1.1 %place.1 = (bf16[48,128,128]{2,1,0:T(8,128)(2,1)}, bf16[24,128]{1,0:T(8,128)(2,1)}) custom-call(bf16[49,128,128]{2,1,0:T(8,128)(2,1)S(1)} %get-tuple-element.7.arr, s32[1,128]{1,0:T(1,128)S(4)} %get-tuple-element.8.inv, bf16[24,128]{1,0:T(8,128)(2,1)S(1)} %get-tuple-element.9.state_in), custom_call_target="tpu_custom_call" | custom-call | tf_op jit(solution)/shard_map/place/pallas_call | solution.py:744
